TPU v7x, 32 devices: a whole 2x2x4 slice. The times are simulated.
32 devices in a mesh: fsdp: 4 (over y, x), ctx: 4 (over z), tp: 2 (over core).
Axes of the slice: x: 2, y: 2, z: 4, core: 2. Of those that a mesh axis runs over, the one named last changes fastest.
Arguments:
- tokens: bfloat16 [4, 512, 2560], P('fsdp', 'ctx'), may hold values from -6 to 6
- segment_ids: int32 [4, 512], P('fsdp'), may hold values from 0 to 1, never falling along the last dimension, each value on 1 to 511 neighbouring positions
- w_query: bfloat16 [2560, 2560], P('fsdp', 'tp'), may hold values from -0.125 to 0.125
- w_keyval: bfloat16 [2560, 512], P('fsdp'), may hold values from -0.125 to 0.125
- w_out: bfloat16 [2560, 2560], P('tp', 'fsdp'), may hold values from -1 to 1
- w_gate: bfloat16 [2560, 7680], P('fsdp', 'tp'), may hold values from -0.125 to 0.125
- w_up: bfloat16 [2560, 7680], P('fsdp', 'tp'), may hold values from -0.125 to 0.125
- w_down: bfloat16 [7680, 2560], P('tp', 'fsdp'), may hold values from -0.0625 to 0.0625
- gain_attn: bfloat16 [2560], P('fsdp'), may hold values from 0.5 to 1.5
- gain_ffn: bfloat16 [2560], P('fsdp'), may hold values from 0.5 to 1.5
- cotangent: bfloat16 [4, 512, 2560], P('fsdp', 'ctx'), may hold values from -6 to 6
Outputs:
- out: bfloat16 [4, 512, 2560], P('fsdp', 'ctx')
- grad_tokens: float32 [4, 512, 2560], P('fsdp', 'ctx')
- grad_w_query: float32 [2560, 2560], P('fsdp', 'tp')
- grad_w_keyval: float32 [2560, 512], P('fsdp')
- grad_w_out: float32 [2560, 2560], P('tp', 'fsdp')
- grad_w_gate: float32 [2560, 7680], P('fsdp', 'tp')
- grad_w_up: float32 [2560, 7680], P('fsdp', 'tp')
- grad_w_down: float32 [7680, 2560], P('tp', 'fsdp')
- grad_gain_attn: float32 [2560], P('fsdp')
- grad_gain_ffn: float32 [2560], P('fsdp')
Inputs may be any that keep to these rules, and one draw needn't show every extreme that they name: `segment_ids`: in each packed row the segment numbers never fall and start at 0; every number up to 1 is used; a segment has 1 to 511 tokens.
All inputs are finite; a program needn't handle non-finite values.
Results may differ from a plain program's by a relative error of at most 0.023.
Values may be sent and summed in bfloat16 or wider, within the bound.
A program may use at most 384 MiB of HBM per device.

v0:
```python
import functools

import jax
import jax.numpy as jnp
from jax import lax
from jax.experimental import pallas as pl
from jax.experimental.pallas import tpu as pltpu
from jax.sharding import PartitionSpec as P


HD = 256
NEGATIVE = -1e30
BF = jnp.bfloat16
F32 = jnp.float32
MESH = pl.DeviceIdType.MESH


def rms_scale(value, gain):
    return value * lax.rsqrt(jnp.mean(value * value, axis=-1, keepdims=True) + 1e-06) * gain


def rotate(value, cosine, sine):
    quarter = value.shape[-1] // 4
    first = value[..., :quarter]
    second = value[..., quarter : 2 * quarter]
    rest = value[..., 2 * quarter :]
    return jnp.concatenate(
        [first * cosine - second * sine, second * cosine + first * sine, rest], axis=-1
    )


def unrotate(value, cosine, sine):
    return rotate(value, cosine, -sine)


def matmul(left, right):
    return jnp.dot(left, right, preferred_element_type=F32)


def times_transposed(left, right):
    return lax.dot_general(left, right, (((1,), (1,)), ((), ())), preferred_element_type=F32)


def transposed_times(left, right):
    return lax.dot_general(left, right, (((0,), (0,)), ((), ())), preferred_element_type=F32)


def geglu(gate_in, up_in):
    return jax.nn.gelu(gate_in, approximate=True) * up_in


def swap(value, axis, size, k):
    return lax.ppermute(value, axis, [(i, i ^ k) for i in range(size)])


def per_device(
    sizes,
    tokens,
    segment_ids,
    w_query,
    w_keyval,
    w_out,
    w_gate,
    w_up,
    w_down,
    gain_attn,
    gain_ffn,
    cotangent,
):
    nf, nc, nt = sizes
    fi, ci, ti = lax.axis_index("fsdp"), lax.axis_index("ctx"), lax.axis_index("tp")
    rows = tokens.shape[1]
    depth = tokens.shape[2]
    slab = depth // nf
    half = depth // nt
    heads = w_query.shape[1] // HD
    qcols = heads * HD
    units = w_gate.shape[1] // nc
    scale = HD ** (-0.5)

    def cut(value, start, size, axis):
        return lax.dynamic_slice_in_dim(value, start, size, axis)

    def all_to_all_blocks(blocks, axis, size):
        return [blocks[0]] + [swap(blocks[k], axis, size, k) for k in range(1, size)]

    def gather_blocks(value, axis, size):
        return [value] + [swap(value, axis, size, k) for k in range(1, size)]

    def absolute(blocks, index, axis):
        stacked = jnp.stack(blocks)
        size = len(blocks)
        return jnp.concatenate(
            [lax.dynamic_index_in_dim(stacked, j ^ index, 0, keepdims=False) for j in range(size)],
            axis=axis,
        )

    def rows_to_slabs(value):
        blocks = [cut(value, (fi ^ k) * slab, slab, 1) for k in range(nf)]
        return jnp.concatenate(all_to_all_blocks(blocks, "fsdp", nf), axis=0)

    def slabs_to_rows(value):
        blocks = list(value.reshape(nf, rows, slab))
        return absolute(all_to_all_blocks(blocks, "fsdp", nf), fi, 1)

    def reduce_rows(value, width):
        blocks = list(value.reshape(nf, rows, width))
        got = all_to_all_blocks(blocks, "fsdp", nf)
        return sum(block.astype(F32) for block in got)

    def gather_rows(value):
        return jnp.concatenate(gather_blocks(value, "fsdp", nf), axis=0)

    def both_halves(mine, axis):
        other = swap(mine, "tp", nt, 1)
        return jnp.where(
            ti == 0,
            jnp.concatenate([mine, other], axis=axis),
            jnp.concatenate([other, mine], axis=axis),
        )

    def tp_sum(value):
        low = value.astype(BF)
        return low.astype(F32) + swap(low, "tp", nt, 1).astype(F32)

    def gather_ctx(value):
        mine = cut(value, ti * half, half, 1)
        return both_halves(jnp.concatenate(gather_blocks(mine, "ctx", nc), axis=0), 1)

    def reduce_ctx(value):
        low = value.astype(BF)
        keep = cut(low, ti * half, half, 1)
        send = cut(low, (1 - ti) * half, half, 1)
        both = (keep.astype(F32) + swap(send, "tp", nt, 1).astype(F32)).astype(BF)
        got = all_to_all_blocks(list(both.reshape(nc, rows, half)), "ctx", nc)
        return sum(block.astype(F32) for block in got)

    gate_full = lax.all_gather(cut(w_gate, ci * units, units, 1), "fsdp", axis=0, tiled=True)
    up_full = lax.all_gather(cut(w_up, ci * units, units, 1), "fsdp", axis=0, tiled=True)
    down_full = lax.all_gather(
        cut(w_down, ci * units, units, 0).T, "fsdp", axis=0, tiled=True
    )

    gains = jnp.stack([gain_attn, gain_ffn])
    gains = absolute(gather_blocks(gains, "fsdp", nf), fi, 1).astype(F32)
    gain_one, gain_two = gains[0], gains[1]
    inputs = tokens[0].astype(F32)
    incoming = cotangent[0]

    segment_row = segment_ids[0]
    offset = ci * rows
    local_segment = lax.dynamic_slice_in_dim(segment_row, offset, rows, 0)
    local_index = offset + jnp.arange(rows, dtype=jnp.int32)
    earlier = jnp.sum((segment_row[None, :] < local_segment[:, None]).astype(jnp.int32), axis=1)
    position = (local_index - earlier).astype(F32)
    freqs = 10000.0 ** (-(jnp.arange(HD // 4, dtype=F32) * 2.0 / (HD // 2)))
    angle = position[:, None] * freqs[None, :]
    cosine = jnp.cos(angle)
    sine = jnp.sin(angle)

    normed_attn = rms_scale(inputs, gain_one).astype(BF)
    normed_slab = rows_to_slabs(normed_attn)
    kv_half = cut(w_keyval, ti * HD, HD, 1)
    partial = jnp.concatenate(
        [matmul(normed_slab, w_query).astype(BF), matmul(normed_slab, kv_half).astype(BF)], axis=1
    )
    projected = reduce_rows(partial, qcols + HD)
    query = projected[:, :qcols].reshape(rows, heads, HD)
    keyval = projected[:, qcols:]
    query_rows = (
        rotate(query, cosine[:, None, :], sine[:, None, :]).reshape(rows * heads, HD).astype(BF)
    )
    keyval = jnp.where(ti == 0, rotate(keyval, cosine, sine), keyval).astype(BF)
    kv_all = jnp.concatenate(gather_blocks(keyval, "ctx", nc), axis=0)
    kv_other = swap(kv_all, "tp", nt, 1)
    key_all = jnp.where(ti == 0, kv_all, kv_other)
    value_all = jnp.where(ti == 0, kv_other, kv_all)

    key_index = jnp.concatenate(
        [(ci ^ k) * rows + jnp.arange(rows, dtype=jnp.int32) for k in range(nc)]
    )
    key_segment = jnp.concatenate(
        [lax.dynamic_slice_in_dim(segment_row, (ci ^ k) * rows, rows, 0) for k in range(nc)]
    )
    row_index = jnp.repeat(local_index, heads)
    row_segment = jnp.repeat(local_segment, heads)
    mask = (row_segment[:, None] == key_segment[None, :]) & (
        key_index[None, :] <= row_index[:, None]
    )
    scores = jnp.where(mask, times_transposed(query_rows, key_all) * scale, NEGATIVE)
    peak = jnp.max(scores, axis=1, keepdims=True)
    terms = jnp.exp(scores - peak)
    probs = terms / jnp.sum(terms, axis=1, keepdims=True)
    probs_low = probs.astype(BF)
    attended = matmul(probs_low, value_all).reshape(rows, qcols).astype(BF)

    attended_plane = gather_rows(attended)
    branch = tp_sum(matmul(attended_plane, w_out)).astype(BF)
    hidden_state = inputs + slabs_to_rows(branch).astype(F32)
    normed_ffn = rms_scale(hidden_state, gain_two).astype(BF)

    normed_all = gather_ctx(normed_ffn)
    incoming_all = gather_ctx(incoming)
    gate = matmul(normed_all, gate_full)
    upward = matmul(normed_all, up_full)
    d_hidden = matmul(incoming_all, down_full)
    hidden, geglu_pull = jax.vjp(geglu, gate, upward)
    hidden = hidden.astype(BF)
    d_gate, d_up = geglu_pull(d_hidden)
    d_gate = d_gate.astype(BF)
    d_up = d_up.astype(BF)

    def finish(grad, axis):
        low = grad.astype(BF)
        blocks = [cut(low, (fi ^ k) * slab, slab, axis) for k in range(nf)]
        got = all_to_all_blocks(blocks, "fsdp", nf)
        return sum(block.astype(F32) for block in got).astype(BF)

    shard_down = finish(transposed_times(hidden, incoming_all), 1)
    grad_down = lax.all_gather(shard_down, "ctx", axis=0, tiled=True).astype(F32)
    shard_gate = finish(transposed_times(normed_all, d_gate), 0)
    grad_gate = lax.all_gather(shard_gate, "ctx", axis=0, tiled=False)
    shard_up = finish(transposed_times(normed_all, d_up), 0)
    grad_up = lax.all_gather(shard_up, "ctx", axis=0, tiled=False)

    def spread(value):
        return jnp.concatenate([value[j] for j in range(nc)], axis=1).astype(F32)

    grad_gate = spread(grad_gate)
    grad_up = spread(grad_up)

    d_normed_ffn = reduce_ctx(
        times_transposed(d_gate, gate_full) + times_transposed(d_up, up_full)
    ).astype(BF)
    d_normed_ffn = both_halves(d_normed_ffn, 1).astype(F32)
    feed = reduce_ctx(times_transposed(hidden, down_full))
    output = both_halves((cut(hidden_state, ti * half, half, 1) + feed).astype(BF), 1)

    unused, norm_pull = jax.vjp(rms_scale, hidden_state, gain_two)
    d_state_norm, grad_gain_two = norm_pull(d_normed_ffn)
    d_state = incoming.astype(F32) + d_state_norm
    d_branch_slab = rows_to_slabs(d_state.astype(BF))
    grad_out = transposed_times(attended_plane, d_branch_slab)
    d_attended = reduce_rows(times_transposed(d_branch_slab, w_out).astype(BF), qcols)
    d_attended = d_attended.astype(BF).reshape(rows * heads, HD)
    d_probs = times_transposed(d_attended, value_all)
    delta = jnp.sum(probs * d_probs, axis=1, keepdims=True)
    d_scores = (probs * (d_probs - delta)).astype(BF)
    d_rows = matmul(d_scores, key_all) * scale
    d_key = transposed_times(d_scores, query_rows) * scale
    d_value = transposed_times(probs_low, d_attended)
    d_key, d_value = d_key.astype(BF), d_value.astype(BF)
    keep = jnp.where(ti == 0, d_key, d_value)
    send = jnp.where(ti == 0, d_value, d_key)
    d_kv = (keep.astype(F32) + swap(send, "tp", nt, 1).astype(F32)).astype(BF)
    d_kv = sum(
        block.astype(F32)
        for block in all_to_all_blocks(list(d_kv.reshape(nc, rows, HD)), "ctx", nc)
    )
    d_kv = jnp.where(ti == 0, unrotate(d_kv, cosine, sine), d_kv).astype(BF)
    d_query = unrotate(d_rows.reshape(rows, heads, HD), cosine[:, None, :], sine[:, None, :])
    d_query = d_query.reshape(rows, qcols).astype(BF)
    d_plane = gather_rows(jnp.concatenate([d_query, d_kv], axis=1))
    d_query_plane = d_plane[:, :qcols]
    d_kv_plane = d_plane[:, qcols:]
    d_normed = tp_sum(
        times_transposed(d_query_plane, w_query) + times_transposed(d_kv_plane, kv_half)
    ).astype(BF)
    d_normed_attn = slabs_to_rows(d_normed).astype(F32)
    grad_query = transposed_times(normed_slab, d_query_plane)
    grad_kv = transposed_times(normed_slab, d_kv_plane)
    unused, norm_pull_one = jax.vjp(rms_scale, inputs, gain_one)
    d_input_norm, grad_gain_one = norm_pull_one(d_normed_attn)
    grad_inputs = d_state + d_input_norm

    grad_out = lax.psum(grad_out.astype(BF), "ctx").astype(F32)
    grad_query = lax.psum(grad_query.astype(BF), "ctx").astype(F32)
    grad_kv = lax.psum(grad_kv.astype(BF), "ctx")
    grad_kv = both_halves(grad_kv, 1).astype(F32)
    gain_grads = jnp.stack([grad_gain_one, grad_gain_two])
    gain_blocks = [cut(gain_grads, (fi ^ k) * slab, slab, 1) for k in range(nf)]
    gain_grads = sum(all_to_all_blocks(gain_blocks, "fsdp", nf))
    step = 1
    while step < nc:
        gain_grads = gain_grads + swap(gain_grads, "ctx", nc, step)
        step *= 2
    return (
        output[None],
        grad_inputs[None],
        grad_query,
        grad_kv,
        grad_out,
        grad_gate,
        grad_up,
        grad_down,
        gain_grads[0],
        gain_grads[1],
    )


def partners(axis, size):
    me = lax.axis_index(axis)
    flip = me + 1 - 2 * lax.rem(me, 2)
    return [me, flip, lax.rem(me + 2, size), size - 1 - me]


class Wire:
    def __init__(self, send, recv):
        self.send, self.recv, self.count, self.live = send, recv, 0, []

    def __call__(self, src, dst, axis, peer):
        slot = self.count
        self.count += 1
        copy = pltpu.make_async_remote_copy(
            src_ref=src,
            dst_ref=dst,
            send_sem=self.send.at[slot],
            recv_sem=self.recv.at[slot],
            device_id={axis: peer},
            device_id_type=MESH,
        )
        copy.start()
        self.live.append(copy)
        return copy

    def settle(self, copies):
        for copy in copies:
            copy.wait_send()
            self.live = [each for each in self.live if each is not copy]

    def finish(self):
        for copy in self.live:
            copy.wait_send()


def greet(peers):
    barrier = pltpu.get_barrier_semaphore()
    for axis, peer in peers:
        pl.semaphore_signal(barrier, inc=1, device_id={axis: peer}, device_id_type=MESH)
    pl.semaphore_wait(barrier, len(peers))


def wide(value, columns):
    return jnp.concatenate([value] * (columns // value.shape[1]), axis=1)


def nt_dot(left, right):
    return lax.dot_general(left, right, (((1,), (1,)), ((), ())), preferred_element_type=F32)


def tn_dot(left, right):
    return lax.dot_general(left, right, (((0,), (0,)), ((), ())), preferred_element_type=F32)


class Gather:
    def __init__(self, wire, fs, pieces, height, place, own=None):
        self.wire, self.fs, self.pieces, self.height = wire, fs, pieces, height
        self.place, self.own = place, own
        self.arrivals = {}

    def strip(self, p):
        return pl.ds(p * self.height, self.height)

    def send(self, m, p, k):
        target = self.place(m, self.fs[0], self.strip(p))
        source = self.own.at[self.strip(p), :] if self.own is not None else target
        self.arrivals[m, p, k] = self.wire(source, target, "fsdp", self.fs[k])

    def pass_on(self, m, p, k, to):
        self.arrivals.pop((m, p, k)).wait_recv()
        target = self.place(m, self.fs[k], self.strip(p))
        self.arrivals[m, p, 3] = self.wire(target, target, "fsdp", self.fs[to])

    def steps(self, which, prepare):
        half = self.pieces // 2
        for m in which:
            prepare(m)
            for i in range(half):
                self.send(m, i, 1)
                self.send(m, half + i, 2)
                yield
            for i in range(half):
                self.pass_on(m, half + i, 2, 1)
                self.pass_on(m, i, 1, 2)
                yield
            for i in range(half):
                self.send(m, half + i, 1)
                self.send(m, i, 2)
                yield

    def settle(self):
        for copy in self.arrivals.values():
            copy.wait_recv()


def gather_kernel(w_down, after, down_full, down_rows, own, send, recv, local):
    del after
    fs = partners("fsdp", 4)
    ci = lax.axis_index("ctx")
    units, slab = down_rows.shape
    load = pltpu.make_async_copy(
        w_down.at[pl.ds(pl.multiple_of(ci * units, 64), units), :], down_rows, local.at[0]
    )
    load.start()
    greet([("fsdp", fs[1]), ("fsdp", fs[2])])
    wire = Wire(send, recv)
    gather = Gather(
        wire, fs, 8, slab // 8, lambda m, index, at: down_full.at[index, at, :], own=own
    )
    keep = pltpu.make_async_copy(own, down_full.at[fs[0]], local.at[1])

    def prepare(m):
        load.wait()
        own[...] = down_rows[...].T
        keep.start()

    for _ in gather.steps((0,), prepare):
        pass
    gather.settle()
    keep.wait()
    wire.finish()


def call_gather(w_down, after):
    units, slab = w_down.shape[0] // 4, w_down.shape[1]
    hbm = pl.BlockSpec(memory_space=pl.ANY)
    return pl.pallas_call(
        gather_kernel,
        out_shape=jax.ShapeDtypeStruct((4, slab, units), BF),
        in_specs=[hbm] * 2,
        out_specs=hbm,
        scratch_shapes=[
            pltpu.VMEM((units, slab), BF),
            pltpu.VMEM((slab, units), BF),
            pltpu.SemaphoreType.DMA((24,)),
            pltpu.SemaphoreType.DMA((24,)),
            pltpu.SemaphoreType.DMA((2,)),
        ],
        compiler_params=pltpu.CompilerParams(collective_id=2, has_side_effects=True),
        cost_estimate=pl.CostEstimate(flops=0, bytes_accessed=120_000_000, transcendentals=0),
        name="gather_down",
    )(w_down, after)


def forward_kernel(
    heads,
    tok,
    cot,
    gains,
    cos,
    sin,
    keep,
    w_q,
    w_kv,
    w_o,
    w_gate,
    w_up,
    q_rot,
    kv_out,
    probs,
    state,
    gains_all,
    normed_all,
    cot_all,
    gate_full,
    up_full,
    normed_slab,
    att_plane,
    gate,
    upward,
    hidden,
    shard,
    xbuf,
    rbuf,
    part,
    precv,
    kvbuf,
    attbuf,
    obuf,
    orecv,
    bbuf,
    brecv,
    nown,
    grel,
    window,
    wfull,
    nall,
    call,
    parts,
    near,
    far,
    sums,
    send,
    recv,
    local,
):
    fs, cs = partners("fsdp", 4), partners("ctx", 4)
    ci, ti = lax.axis_index("ctx"), lax.axis_index("tp")
    other = 1 - ti
    rows, depth = tok.shape
    slab = depth // 4
    hrows = rows // 2
    qcols = heads * HD
    units = gate_full.shape[2]
    scale = HD ** (-0.5)
    wire = Wire(send, recv)
    locals_ = []

    def keep_local(src, dst):
        copy = pltpu.make_async_copy(src, dst, local.at[len(locals_)])
        copy.start()
        locals_.append(copy)
        return copy

    def lanes(index):
        return pl.ds(pl.multiple_of(index * slab, slab), slab)

    mine = pl.ds(pl.multiple_of(ti * hrows, hrows), hrows)
    first = pl.ds(pl.multiple_of(((ci * units) // 128) * 128, 128), window.shape[2])
    win = [
        keep_local(w_gate.at[:, first], window.at[0]),
        keep_local(w_up.at[:, first], window.at[1]),
    ]
    greet(
        [("fsdp", fs[k]) for k in (1, 2, 3)]
        + [("ctx", cs[k]) for k in (1, 2, 3)]
        + [("tp", other)]
    )

    x_in = [None] * 4
    for k in (1, 2, 3):
        x_in[k] = wire(tok.at[:, lanes(fs[k])], xbuf.at[k], "fsdp", fs[k])
    g_in = [None] * 4
    for k in (1, 2, 3):
        g_in[k] = wire(gains, grel.at[k], "fsdp", fs[k])
    grel[0] = gains[...]
    xbuf[0] = tok[:, lanes(fs[0])]
    x = tok[...].astype(F32)
    r = lax.rsqrt(jnp.sum(x * x, axis=1, keepdims=True) * (1.0 / depth) + 1e-06)
    rbuf[0] = jnp.broadcast_to(r, (rows, 128))
    r_in = [None] * 4
    for k in (1, 2, 3):
        r_in[k] = wire(rbuf.at[0], rbuf.at[k], "fsdp", fs[k])
    c_in = [None] * 4
    for k in (1, 2, 3):
        c_in[k] = wire(cot.at[mine, :], call.at[ci, ti], "ctx", cs[k])
    for half in (0, 1):
        call[ci, half] = cot[half * hrows : (half + 1) * hrows, :]

    odd = units % 128
    pieces = 8
    height = slab // pieces

    def prepare(m):
        win[m].wait()
        if odd:

            @pl.when(lax.rem(ci, 2) == 0)
            def _():
                wfull[m, fs[0]] = window[m, :, 0:units]

            @pl.when(lax.rem(ci, 2) == 1)
            def _():
                wfull[m, fs[0]] = window[m, :, odd : odd + units]
        else:
            wfull[m, fs[0]] = window[m, :, 0:units]

    gather = Gather(wire, fs, pieces, height, lambda m, index, at: wfull.at[m, index, at, :])
    schedule = gather.steps((0, 1), prepare)

    def bulk(count):
        for _ in range(count):
            next(schedule, None)

    bulk(BULK[0])
    gain_one = gains[0:1, :]
    kv_half = w_kv[:, pl.ds(pl.multiple_of(ti * HD, HD), HD)]
    p_in = [None] * 4
    for k in range(4):
        if k:
            x_in[k].wait_recv()
            r_in[k].wait_recv()
        normed = (xbuf[k].astype(F32) * wide(rbuf[k], slab) * gain_one).astype(BF)
        normed_slab[k] = normed
        part[k, :, 0:qcols] = jnp.dot(normed, w_q[...], preferred_element_type=F32).astype(BF)
        part[k, :, qcols:] = jnp.dot(normed, kv_half, preferred_element_type=F32).astype(BF)
        if k:
            p_in[k] = wire(part.at[k], precv.at[k], "fsdp", fs[k])
    bulk(BULK[1])
    for k in (1, 2, 3):
        p_in[k].wait_recv()

    def total(start, size):
        out = part[0, :, start : start + size].astype(F32)
        for k in (1, 2, 3):
            out += precv[k, :, start : start + size].astype(F32)
        return out

    c, s = cos[...], sin[...]
    zero = (1 - ti).astype(F32)
    kvbuf[ti, 0] = turn(total(qcols, HD), c * zero + (1.0 - zero), s * zero).astype(BF)
    kv_in = [None] * 4
    for k in (1, 2, 3):
        kv_in[k] = wire(kvbuf.at[ti, 0], kvbuf.at[ti, k], "ctx", cs[k])
    kv_side = [wire(kvbuf.at[ti, 0], kvbuf.at[ti, 0], "tp", other)]
    for h in range(heads):
        q_rot[:, h * HD : (h + 1) * HD] = turn(total(h * HD, HD), c, s).astype(BF)
    bulk(BULK[2])
    for k in (1, 2, 3):
        kv_in[k].wait_recv()
        kv_side.append(wire(kvbuf.at[ti, k], kvbuf.at[ti, k], "tp", other))
    for copy in kv_side:
        copy.wait_recv()
    length = 4 * rows
    keys = kvbuf[0].reshape(length, HD)
    values = kvbuf[1].reshape(length, HD)
    kv_out[...] = kvbuf[...]
    seen = keep[...] > 0.5
    for h in range(heads):
        sc = nt_dot(q_rot[:, h * HD : (h + 1) * HD], keys) * scale
        sc = jnp.where(seen, sc, NEGATIVE)
        e = jnp.exp(sc - jnp.max(sc, axis=1, keepdims=True))
        p = e / jnp.sum(e, axis=1, keepdims=True)
        probs[h] = p
        attbuf[0, :, h * HD : (h + 1) * HD] = jnp.dot(
            p.astype(BF), values, preferred_element_type=F32
        ).astype(BF)
    a_in = [None] * 4
    for k in (1, 2, 3):
        a_in[k] = wire(attbuf.at[0], attbuf.at[k], "fsdp", fs[k])
    bulk(BULK[3])
    c_side = []
    for k in (1, 2, 3):
        c_in[k].wait_recv()
        c_side.append(wire(call.at[cs[k], ti], call.at[cs[k], ti], "tp", other))
    o_in = []
    for k in range(4):
        if k:
            a_in[k].wait_recv()
        att_plane[k] = attbuf[k]
        block = jnp.dot(attbuf[k], w_o[...], preferred_element_type=F32).astype(BF)
        obuf[k, 0] = block[0:hrows]
        obuf[k, 1] = block[hrows:rows]
        o_in.append(wire(obuf.at[k, other], orecv.at[k], "tp", other))
    b_in = [None] * 4
    for k in (1, 2, 3, 0):
        o_in[k].wait_recv()
        both = (obuf[k, ti].astype(F32) + orecv[k].astype(F32)).astype(BF)
        if k:
            bbuf[k] = both
            b_in[k] = wire(bbuf.at[k], brecv.at[k], "fsdp", fs[k])
        else:
            brecv[0] = both
    bulk(BULK[4])
    for k in (1, 2, 3):
        g_in[k].wait_recv()
    gains_all[...] = grel[...]
    squares = jnp.zeros((hrows, 1), F32)
    for k in range(4):
        if k:
            b_in[k].wait_recv()
        h_new = tok[mine, lanes(fs[k])].astype(F32) + brecv[k].astype(F32)
        state[:, lanes(fs[k])] = h_new
        squares += jnp.sum(h_new * h_new, axis=1, keepdims=True)
    r2 = lax.rsqrt(squares * (1.0 / depth) + 1e-06)
    for k in range(4):
        nown[:, lanes(fs[k])] = (state[:, lanes(fs[k])] * r2 * grel[k, 1:2, :]).astype(BF)
    n_in = [None] * 4
    for k in (1, 2, 3):
        n_in[k] = wire(nown, nall.at[ci, ti], "ctx", cs[k])
    n_side = [wire(nown, nall.at[ci, ti], "tp", other)]
    nall[ci, ti] = nown[...]
    bulk(BULK[5])
    for k in (1, 2, 3):
        n_in[k].wait_recv()
        n_side.append(wire(nall.at[cs[k], ti], nall.at[cs[k], ti], "tp", other))
        bulk(BULK[6])
    bulk(1000)
    gather.settle()
    keep_local(wfull.at[0], gate_full)
    keep_local(wfull.at[1], up_full)
    for k in range(4):
        n_side[k].wait_recv()
        x = nall[cs[k]].reshape(rows, depth)
        at = pl.ds(pl.multiple_of(cs[k] * rows, rows), rows)
        g = jnp.dot(x, wfull[0].reshape(depth, units), preferred_element_type=F32)
        u = jnp.dot(x, wfull[1].reshape(depth, units), preferred_element_type=F32)
        gate[at, :] = g
        upward[at, :] = u
        cdf = 0.5 * (1.0 + jnp.tanh(0.7978845608028654 * (g + 0.044715 * (g * g * g))))
        hidden[at, :] = (g * cdf * u).astype(BF)
    keep_local(nall, normed_all)
    for copy in c_side:
        copy.wait_recv()
    keep_local(call, cot_all)
    product = Product(wire, True, hidden, call, shard, parts, near, far, sums)
    product.start()
    product.middle()
    product.end()
    for copy in locals_[2:]:
        copy.wait()
    wire.finish()


BULK = (3, 4, 3, 3, 3, 6, 1)


def call_forward(heads, tok, cot, gains, cos, sin, keep, w_q, w_kv, w_o, w_gate, w_up):
    rows, depth = tok.shape
    slab, hrows, qcols, length = depth // 4, rows // 2, heads * HD, 4 * rows
    units = w_gate.shape[1] // 4
    reach = -(-(units + units % 128) // 128) * 128
    shape = jax.ShapeDtypeStruct
    vmem = pl.BlockSpec(memory_space=pltpu.VMEM)
    hbm = pl.BlockSpec(memory_space=pl.ANY)
    pcols = qcols + HD
    sizes = product_sizes(True, slab, units)
    pair = [pltpu.VMEM((2, *size), BF) for size in sizes]
    single = [pltpu.VMEM(size, BF) for size in sizes]
    return pl.pallas_call(
        functools.partial(forward_kernel, heads),
        out_shape=[
            shape((rows, qcols), BF),
            shape((2, 4, rows, HD), BF),
            shape((heads, rows, length), F32),
            shape((hrows, depth), F32),
            shape((4, 8, slab), F32),
            shape((4, 2, hrows, depth), BF),
            shape((4, 2, hrows, depth), BF),
            shape((4, slab, units), BF),
            shape((4, slab, units), BF),
            shape((4, rows, slab), BF),
            shape((4, rows, qcols), BF),
            shape((length, units), F32),
            shape((length, units), F32),
            shape((length, units), BF),
            shape((units, slab), BF),
        ],
        in_specs=[vmem] * 9 + [hbm] * 2,
        out_specs=[vmem] * 5 + [hbm] * 4 + [vmem] * 6,
        scratch_shapes=[
            pltpu.VMEM((4, rows, slab), BF),
            pltpu.VMEM((4, rows, 128), F32),
            pltpu.VMEM((4, rows, pcols), BF),
            pltpu.VMEM((4, rows, pcols), BF),
            pltpu.VMEM((2, 4, rows, HD), BF),
            pltpu.VMEM((4, rows, qcols), BF),
            pltpu.VMEM((4, 2, hrows, slab), BF),
            pltpu.VMEM((4, hrows, slab), BF),
            pltpu.VMEM((4, hrows, slab), BF),
            pltpu.VMEM((4, hrows, slab), BF),
            pltpu.VMEM((hrows, depth), BF),
            pltpu.VMEM((4, 8, slab), F32),
            pltpu.VMEM((2, slab, reach), BF),
            pltpu.VMEM((2, 4, slab, units), BF),
            pltpu.VMEM((4, 2, hrows, depth), BF),
            pltpu.VMEM((4, 2, hrows, depth), BF),
            list(pair),
            list(pair),
            list(single),
            list(single),
            pltpu.SemaphoreType.DMA((132,)),
            pltpu.SemaphoreType.DMA((132,)),
            pltpu.SemaphoreType.DMA((12,)),
        ],
        compiler_params=pltpu.CompilerParams(
            collective_id=1, has_side_effects=True, vmem_limit_bytes=67_043_328
        ),
        cost_estimate=pl.CostEstimate(
            flops=2 * length * slab * (2 * qcols + HD), bytes_accessed=400_000_000, transcendentals=0
        ),
        name="attention_forward",
    )(tok, cot, gains, cos, sin, keep, w_q, w_kv, w_o, w_gate, w_up)


class Product:
    def __init__(self, wire, flip, left, right, shard, mine, near, far, sums):
        self.wire, self.flip, self.left, self.right, self.shard = wire, flip, left, right, shard
        self.mine, self.near, self.far, self.sums = mine, near, far, sums
        self.fs = partners("fsdp", 4)
        self.slab = shard.shape[1] if flip else shard.shape[0]
        units = shard.shape[0] if flip else shard.shape[1]
        cut = 128 * ((units + 255) // 256)
        self.spans = ((0, cut), (cut, units - cut))
        self.first, self.second = (1, 2), (2, 1)
        self.one, self.two = {}, {}

    def piece(self, k, half):
        start, size = self.spans[half]
        block = pl.ds(pl.multiple_of(self.fs[k] * self.slab, self.slab), self.slab)
        if self.flip:
            right = self.right[..., block]
            right = right.reshape(-1, right.shape[-1])
            return tn_dot(self.left[:, start : start + size], right)
        return tn_dot(self.left[:, block], self.right[:, start : start + size])

    def start(self):
        for slot in (0, 1):
            for half in (0, 1):
                k = 3 if slot == 0 else self.first[half]
                self.mine[half][slot] = self.piece(k, half).astype(BF)
                self.one[half, slot] = self.wire(
                    self.mine[half].at[slot],
                    self.near[half].at[slot],
                    "fsdp",
                    self.fs[self.first[half]],
                )

    def middle(self):
        for half in (0, 1):
            own = self.piece(self.second[half], half)
            self.one[half, 0].wait_recv()
            self.sums[half][...] = (own + self.near[half][0].astype(F32)).astype(BF)
            self.two[half] = self.wire(
                self.sums[half], self.far[half], "fsdp", self.fs[self.second[half]]
            )

    def end(self):
        for half in (0, 1):
            start, size = self.spans[half]
            own = self.piece(0, half)
            self.one[half, 1].wait_recv()
            own += self.near[half][1].astype(F32)
            self.two[half].wait_recv()
            own += self.far[half][...].astype(F32)
            if self.flip:
                self.shard[start : start + size, :] = own.astype(BF)
            else:
                self.shard[:, start : start + size] = own.astype(BF)


def product_sizes(flip, slab, units):
    cut = 128 * ((units + 255) // 256)
    return [(size, slab) if flip else (slab, size) for size in (cut, units - cut)]


def turn(value, c, s):
    front = value[:, 0:128]
    return jnp.concatenate(
        [front * c + pltpu.roll(front, 64, 1) * s, value[:, 128:256]], axis=1
    )


class Line:
    def __init__(self, own, inbox, outbox, total, send, recv):
        self.own, self.inbox, self.outbox, self.total = own, inbox, outbox, total
        self.send, self.recv = send, recv
        self.ci = lax.axis_index("ctx")

    def copy(self, way, u):
        step = 1 if way == 0 else 3
        return pltpu.make_async_remote_copy(
            src_ref=self.outbox.at[way, u - 1 + way],
            dst_ref=self.inbox.at[way, u - 1 + way],
            send_sem=self.send.at[way, u - 1 + way],
            recv_sem=self.recv.at[way, u - 1 + way],
            device_id={"ctx": lax.rem(self.ci + step, 4)},
            device_id_type=MESH,
        )

    def sends(self, way, u):
        return self.ci < u if way == 0 else self.ci > u

    def fed(self, way):
        return self.ci > 0 if way == 0 else self.ci < 3

    def lead(self):
        for step in range(3):
            for way, u in ((0, 3 - step), (1, step)):

                @pl.when(jnp.logical_and(self.sends(way, u), jnp.logical_not(self.fed(way))))
                def _():
                    self.outbox[way, u - 1 + way] = self.own(u).astype(BF)
                    self.copy(way, u).start()

    def push(self, step):
        for way, u in ((0, 3 - step), (1, step)):

            @pl.when(jnp.logical_and(self.sends(way, u), self.fed(way)))
            def _():
                self.copy(way, u).wait_recv()
                slot = u - 1 + way
                self.outbox[way, slot] = (
                    self.own(u) + self.inbox[way, slot].astype(F32)
                ).astype(BF)
                self.copy(way, u).start()

    def collect(self):
        self.total[...] = self.own(self.ci)
        for way in (0, 1):

            @pl.when(self.fed(way))
            def _():
                self.copy(way, self.ci).wait_recv()
                self.total[...] += self.inbox[way, self.ci - 1 + way].astype(F32)

    def drain(self):
        for way in (0, 1):
            for u in range(1 - way, 4 - way):

                @pl.when(self.sends(way, u))
                def _():
                    self.copy(way, u).wait_send()


def line_scratch(*form):
    return [
        pltpu.VMEM((2, 3, *form), BF),
        pltpu.VMEM((2, 3, *form), BF),
        pltpu.VMEM(form, F32),
        pltpu.SemaphoreType.DMA((2, 3)),
        pltpu.SemaphoreType.DMA((2, 3)),
    ]


class Spread:
    def __init__(self, own, full, pieces, send, recv, local):
        self.own, self.full, self.pieces = own, full, pieces
        self.send, self.recv = send, recv
        self.height = own.shape[0] // pieces
        self.cs = partners("ctx", 4)
        self.ci = self.cs[0]
        self.inner = jnp.logical_and(self.ci > 0, self.ci < 3)
        self.local = pltpu.make_async_copy(own, full.at[self.ci], local)

    def strip(self, p):
        return pl.ds(p * self.height, self.height)

    def copy(self, kind, p, source, peer):
        place = self.full.at[source, self.strip(p), :]
        src = self.own.at[self.strip(p), :] if kind < 2 else place
        slot = (0, 1, 2, 1, 2)[kind]
        return pltpu.make_async_remote_copy(
            src_ref=src,
            dst_ref=place,
            send_sem=self.send.at[kind, p],
            recv_sem=self.recv.at[slot, p],
            device_id={"ctx": peer},
            device_id_type=MESH,
        )

    def out(self, kind, p):
        cs = self.cs
        source = (cs[0], cs[0], cs[1], cs[3], cs[2])[kind]
        peer = (cs[1], cs[3], cs[3], cs[1], cs[1])[kind]
        return self.copy(kind, p, source, peer)

    def arrived(self, slot, p):
        self.copy((0, 1, 2)[slot], p, self.ci, self.cs[1]).wait_recv()

    def begin(self):
        self.local.start()

    def give(self, p):
        self.out(0, p).start()

        @pl.when(self.inner)
        def _():
            self.out(1, p).start()

    def hand_on(self, p):
        @pl.when(self.inner)
        def _():
            self.arrived(0, p)
            self.out(2, p).start()
            self.arrived(1, p)
            self.out(3, p).start()

    def hand_far(self, p):
        @pl.when(self.inner)
        def _():
            self.arrived(2, p)
            self.out(4, p).start()

    def close(self):
        for p in range(self.pieces):

            @pl.when(jnp.logical_not(self.inner))
            def _():
                for slot in range(3):
                    self.arrived(slot, p)

            self.out(0, p).wait_send()

            @pl.when(self.inner)
            def _():
                for kind in range(1, 5):
                    self.out(kind, p).wait_send()

        self.local.wait()


def spread_scratch(pieces):
    return [
        pltpu.SemaphoreType.DMA((5, pieces)),
        pltpu.SemaphoreType.DMA((3, pieces)),
        pltpu.SemaphoreType.DMA,
    ]


def units_line(wire, part, side, line_refs, ti):
    other = 1 - ti
    side_in = [wire(part.at[u, other], side.at[u], "tp", other) for u in range(4)]
    for copy in side_in:
        copy.wait_recv()
    return Line(lambda u: part[u, ti].astype(F32) + side[u].astype(F32), *line_refs)


def backward_kernel(
    heads,
    dn,
    cot,
    state,
    gains_all,
    probs,
    q_rot,
    kv,
    cos,
    sin,
    w_o,
    normed,
    att,
    normed_all,
    d_gate,
    d_up,
    after,
    d_state,
    gain_part,
    dq_plane,
    dkv_plane,
    weight_grads,
    gate_all,
    up_all,
    side,
    dbuf,
    dslab,
    dpart,
    dfar,
    dkv2,
    kvt,
    zk,
    zfar,
    dqbuf,
    dkvbuf,
    dk_acc,
    dv_acc,
    own_out,
    own_query,
    row_refs,
    out_refs,
    query_refs,
    parts,
    sums,
    gate_recv,
    up_recv,
    shard_gate,
    shard_up,
    gate_sems,
    up_sems,
    send,
    recv,
    local,
):
    del after
    fs, cs = partners("fsdp", 4), partners("ctx", 4)
    ti = lax.axis_index("tp")
    other = 1 - ti
    hrows, depth = state.shape
    rows = 2 * hrows
    slab = depth // 4
    length = 4 * rows
    scale = HD ** (-0.5)
    greet(
        [("fsdp", fs[k]) for k in (1, 2, 3)]
        + [("ctx", cs[k]) for k in (1, 2, 3)]
        + [("tp", other)]
    )
    wire = Wire(send, recv)
    mine = pl.ds(pl.multiple_of(ti * hrows, hrows), hrows)

    def lanes(index):
        return pl.ds(pl.multiple_of(index * slab, slab), slab)

    gate = Product(wire, False, normed_all, d_gate, shard_gate, parts, *gate_recv, sums)
    up = Product(wire, False, normed_all, d_up, shard_up, parts, *up_recv, sums)
    gate_line = Spread(shard_gate, gate_all, PIECES, *gate_sems)
    up_line = Spread(shard_up, up_all, PIECES, *up_sems)
    gate.start()
    line = units_line(wire, dn, side, row_refs, ti)
    line.lead()
    squares = jnp.zeros((hrows, 1), F32)
    for k in range(4):
        u = state[:, lanes(fs[k])]
        squares += jnp.sum(u * u, axis=1, keepdims=True)
    r = lax.rsqrt(squares * (1.0 / depth) + 1e-06)
    gate.middle()
    line.push(0)
    line.push(1)
    gate.end()
    gate_line.begin()
    for p in range(PIECES):
        gate_line.give(p)
    line.push(2)
    line.collect()
    inner = jnp.zeros((hrows, 1), F32)
    for k in range(4):
        at = lanes(fs[k])
        inner += jnp.sum(
            state[:, at] * gains_all[k, 1:2, :] * line.total[:, at], axis=1, keepdims=True
        )
    pull = r * r * r * (inner * (1.0 / depth))
    d_in = {}
    d_side = {}
    gain_part[...] = jnp.zeros_like(gain_part)
    for k in (1, 2, 3, 0):
        at = lanes(fs[k])
        u, d = state[:, at], line.total[:, at]
        ds = cot[mine, at].astype(F32) + (r * (gains_all[k, 1:2, :] * d) - u * pull)
        d_state[:, at] = ds
        if k:
            dbuf[k] = ds.astype(BF)
            d_in[k] = wire(dbuf.at[k], dslab.at[k, ti], "fsdp", fs[k])
        else:
            dslab[0, ti] = ds.astype(BF)
            d_side[0] = wire(dslab.at[0, ti], dslab.at[0, ti], "tp", other)
        gain_part[k, 1:2, :] = jnp.sum(u * r * d, axis=0, keepdims=True)
    for k in (1, 2, 3):
        d_in[k].wait_recv()
        d_side[k] = wire(dslab.at[k, ti], dslab.at[k, ti], "tp", other)
    a_in = {}
    for k in (1, 2, 3, 0):
        d_side[k].wait_recv()
        block = dslab[k].reshape(rows, slab)
        dpart[k] = nt_dot(block, w_o[...]).astype(BF)
        if k:
            a_in[k] = wire(dpart.at[k], dfar.at[k], "fsdp", fs[k])
    wire.settle(list(gate.one.values()) + list(gate.two.values()))
    up.start()
    keys = kv[0].reshape(length, HD)
    values = kv[1].reshape(length, HD)
    c, s = cos[...], sin[...]
    quarter = heads * HD // 4
    branch = dslab[...].reshape(length, slab)
    for u in range(4):
        columns = att[:, :, u * quarter : (u + 1) * quarter].reshape(length, quarter)
        own_out[u] = tn_dot(columns, branch).astype(BF)
    out_line = Line(lambda u: own_out[u].astype(F32), *out_refs)
    for k in (1, 2, 3):
        a_in[k].wait_recv()
    for h in range(heads):
        at = slice(h * HD, (h + 1) * HD)
        d = dpart[0, :, at].astype(F32)
        for k in (1, 2, 3):
            d += dfar[k, :, at].astype(F32)
        d = d.astype(BF)
        p = probs[h]
        dp = nt_dot(d, values)
        delta = jnp.sum(p * dp, axis=1, keepdims=True)
        dsc = (p * (dp - delta)).astype(BF)
        dq = jnp.dot(dsc, keys, preferred_element_type=F32) * scale
        dqbuf[0, :, at] = turn(dq, c, -s).astype(BF)
        dk = tn_dot(dsc, q_rot[:, at])
        dv = tn_dot(p.astype(BF), d)
        if h == 0:
            dk_acc[...] = dk
            dv_acc[...] = dv
        else:
            dk_acc[...] += dk
            dv_acc[...] += dv
    dkv2[0] = (dk_acc[...] * scale).astype(BF).reshape(4, rows, HD)
    dkv2[1] = dv_acc[...].astype(BF).reshape(4, rows, HD)
    k_side = wire(dkv2.at[other], kvt, "tp", other)
    q_in = {}
    for k in (1, 2, 3):
        q_in[k] = wire(dqbuf.at[0], dqbuf.at[k], "fsdp", fs[k])
    k_side.wait_recv()
    z_in = {}
    for k in (1, 2, 3):
        zk[k] = (dkv2[ti, k].astype(F32) + kvt[k].astype(F32)).astype(BF)
        z_in[k] = wire(zk.at[k], zfar.at[k], "ctx", cs[k])
    for p in range(PIECES // 2):
        gate_line.hand_on(p)
    out_line.lead()
    own = dkv2[ti, 0].astype(F32) + kvt[0].astype(F32)
    for k in (1, 2, 3):
        z_in[k].wait_recv()
        own += zfar[k].astype(F32)
    zero = (1 - ti).astype(F32)
    dkvbuf[0] = turn(own, c * zero + (1.0 - zero), -s * zero).astype(BF)
    v_in = {}
    for k in (1, 2, 3):
        v_in[k] = wire(dkvbuf.at[0], dkvbuf.at[k], "fsdp", fs[k])
    up.middle()
    for p in range(PIECES // 2, PIECES):
        gate_line.hand_on(p)
    out_line.push(0)
    for k in (1, 2, 3):
        q_in[k].wait_recv()
    slabs = normed[...].reshape(length, slab)
    for u in (3, 0, 2, 1):
        columns = dqbuf[:, :, u * quarter : (u + 1) * quarter].reshape(length, quarter)
        own_query[u, 0:quarter] = tn_dot(columns, slabs).astype(BF)
    for k in (1, 2, 3):
        v_in[k].wait_recv()
    keep_q = pltpu.make_async_copy(dqbuf, dq_plane, local.at[0])
    keep_v = pltpu.make_async_copy(dkvbuf, dkv_plane, local.at[1])
    keep_q.start()
    keep_v.start()
    for u in (3, 0, 2, 1):
        columns = dkvbuf[:, :, u * (HD // 4) : (u + 1) * (HD // 4)].reshape(length, HD // 4)
        own_query[u, quarter:] = tn_dot(columns, slabs).astype(BF)
    query_line = Line(lambda u: own_query[u].astype(F32), *query_refs)
    query_line.lead()
    for p in range(PIECES // 2):
        gate_line.hand_far(p)
    up.end()
    up_line.begin()
    for p in range(PIECES // 2):
        up_line.give(p)
    out_line.push(1)
    query_line.push(0)
    for p in range(PIECES // 2, PIECES):
        gate_line.hand_far(p)
    for p in range(PIECES // 2, PIECES):
        up_line.give(p)
    out_line.push(2)
    query_line.push(1)
    query_line.push(2)
    for p in range(PIECES):
        up_line.hand_on(p)
    out_line.collect()
    weight_grads[0:quarter, :] = out_line.total[...].astype(BF)
    query_line.collect()
    weight_grads[quarter:, :] = query_line.total[...].astype(BF)
    for p in range(PIECES):
        up_line.hand_far(p)
    gate_line.close()
    up_line.close()
    for each in (line, out_line, query_line):
        each.drain()
    keep_q.wait()
    keep_v.wait()
    wire.finish()


PIECES = 4


def call_backward(
    heads, dn, cot, state, gains_all, probs, q_rot, kv, cos, sin, w_o, normed, att, normed_all, d_gate, d_up, after
):
    hrows, depth = state.shape
    rows, slab, qcols = 2 * hrows, depth // 4, heads * HD
    length = 4 * rows
    units = d_gate.shape[1]
    sizes = product_sizes(False, slab, units)
    pair = [pltpu.VMEM((2, *size), BF) for size in sizes]
    single = [pltpu.VMEM(size, BF) for size in sizes]
    shape = jax.ShapeDtypeStruct
    vmem = pl.BlockSpec(memory_space=pltpu.VMEM)
    hbm = pl.BlockSpec(memory_space=pl.ANY)
    return pl.pallas_call(
        functools.partial(backward_kernel, heads),
        out_shape=[
            shape((hrows, depth), F32),
            shape((4, 8, slab), F32),
            shape((4, rows, qcols), BF),
            shape((4, rows, HD), BF),
            shape((qcols // 2 + HD // 4, slab), BF),
            shape((4, slab, units), BF),
            shape((4, slab, units), BF),
        ],
        in_specs=[vmem] * 15 + [hbm],
        out_specs=[vmem] * 2 + [hbm] * 2 + [vmem] + [hbm] * 2,
        scratch_shapes=[
            pltpu.VMEM((4, hrows, depth), BF),
            pltpu.VMEM((4, hrows, slab), BF),
            pltpu.VMEM((4, 2, hrows, slab), BF),
            pltpu.VMEM((4, rows, qcols), BF),
            pltpu.VMEM((4, rows, qcols), BF),
            pltpu.VMEM((2, 4, rows, HD), BF),
            pltpu.VMEM((4, rows, HD), BF),
            pltpu.VMEM((4, rows, HD), BF),
            pltpu.VMEM((4, rows, HD), BF),
            pltpu.VMEM((4, rows, qcols), BF),
            pltpu.VMEM((4, rows, HD), BF),
            pltpu.VMEM((length, HD), F32),
            pltpu.VMEM((length, HD), F32),
            pltpu.VMEM((4, qcols // 4, slab), BF),
            pltpu.VMEM((4, (qcols + HD) // 4, slab), BF),
            line_scratch(hrows, depth),
            line_scratch(qcols // 4, slab),
            line_scratch((qcols + HD) // 4, slab),
            list(pair),
            list(single),
            [list(pair), list(single)],
            [list(pair), list(single)],
            pltpu.VMEM((slab, units), BF),
            pltpu.VMEM((slab, units), BF),
            spread_scratch(PIECES),
            spread_scratch(PIECES),
            pltpu.SemaphoreType.DMA((48,)),
            pltpu.SemaphoreType.DMA((48,)),
            pltpu.SemaphoreType.DMA((2,)),
        ],
        compiler_params=pltpu.CompilerParams(
            collective_id=5, has_side_effects=True, vmem_limit_bytes=67_043_328
        ),
        cost_estimate=pl.CostEstimate(
            flops=2 * length * slab * qcols, bytes_accessed=300_000_000, transcendentals=0
        ),
        name="attention_backward",
    )(dn, cot, state, gains_all, probs, q_rot, kv, cos, sin, w_o, normed, att, normed_all, d_gate, d_up, after)


STRIP = 80


def conversions(sources, targets, inbuf, outbuf, in_sems, out_sems):
    jobs = []
    for which in (0, 1):
        for p in range(sources[which].shape[1] // STRIP):
            jobs.append((which, p))
    for p in range(sources[2].shape[0] // (4 * STRIP)):
        jobs.append((2, p))

    def load(n):
        which, p = jobs[n]
        slot = n % 2
        if which < 2:
            source = sources[which].at[:, pl.ds(p * STRIP, STRIP), :]
            return pltpu.make_async_copy(source, inbuf[0].at[slot], in_sems.at[slot])
        source = sources[2].at[pl.ds(p * 4 * STRIP, 4 * STRIP), :]
        return pltpu.make_async_copy(source, inbuf[1].at[slot], in_sems.at[slot])

    def store(n):
        which, p = jobs[n]
        slot = n % 2
        if which < 2:
            target = targets[which].at[pl.ds(p * STRIP, STRIP), :]
            return pltpu.make_async_copy(outbuf[0].at[slot], target, out_sems.at[slot])
        target = targets[2].at[pl.ds(p * 4 * STRIP, 4 * STRIP), :]
        return pltpu.make_async_copy(outbuf[1].at[slot], target, out_sems.at[slot])

    load(0).start()
    for n, (which, p) in enumerate(jobs):
        slot = n % 2
        if n + 1 < len(jobs):
            load(n + 1).start()
        load(n).wait()
        if n >= 2:
            store(n - 2).wait()
        if which < 2:
            units = sources[which].shape[2]
            for j in range(4):
                outbuf[0][slot, :, j * units : (j + 1) * units] = inbuf[0][slot, j].astype(F32)
        else:
            outbuf[1][slot] = inbuf[1][slot].astype(F32)
        store(n).start()
        if n + 1 == len(jobs):
            store(n - 1).wait()
            store(n).wait()
        yield


def convert_kernel(gate_all, up_all, down_all, grad_gate, grad_up, grad_down, inbuf, outbuf, in_sems, out_sems):
    steps = conversions(
        (gate_all, up_all, down_all), (grad_gate, grad_up, grad_down), inbuf, outbuf, in_sems, out_sems
    )
    for _ in steps:
        pass


def call_convert(gate_all, up_all, down_all):
    slab, units = gate_all.shape[1:]
    shape = jax.ShapeDtypeStruct
    hbm = pl.BlockSpec(memory_space=pl.ANY)
    return pl.pallas_call(
        convert_kernel,
        out_shape=[
            shape((slab, 4 * units), F32),
            shape((slab, 4 * units), F32),
            shape((4 * units, slab), F32),
        ],
        in_specs=[hbm] * 3,
        out_specs=[hbm] * 3,
        scratch_shapes=[
            [pltpu.VMEM((2, 4, STRIP, units), BF), pltpu.VMEM((2, 4 * STRIP, slab), BF)],
            [pltpu.VMEM((2, STRIP, 4 * units), F32), pltpu.VMEM((2, 4 * STRIP, slab), F32)],
            pltpu.SemaphoreType.DMA((2,)),
            pltpu.SemaphoreType.DMA((2,)),
        ],
        cost_estimate=pl.CostEstimate(
            flops=0, bytes_accessed=18 * slab * 4 * units, transcendentals=0
        ),
        name="convert",
    )(gate_all, up_all, down_all)


def finish_kernel(
    part,
    state,
    tok,
    gains_all,
    gain_part,
    d_state,
    dq,
    dkv,
    w_q,
    w_kv,
    after,
    out,
    grad_tok,
    gain_grads,
    side,
    row_refs,
    obuf,
    gbuf,
    pbuf,
    pside,
    dbuf,
    drow,
    gpart,
    gfar,
    gsum,
    gnear,
    send,
    recv,
):
    del after
    fs, cs = partners("fsdp", 4), partners("ctx", 4)
    ti = lax.axis_index("tp")
    other = 1 - ti
    hrows, depth = state.shape
    slab = depth // 4
    greet(
        [("fsdp", fs[k]) for k in (1, 2, 3)]
        + [("ctx", cs[k]) for k in (1, 2, 3)]
        + [("tp", other)]
    )
    wire = Wire(send, recv)
    mine = pl.ds(pl.multiple_of(ti * hrows, hrows), hrows)

    def lanes(index):
        return pl.ds(pl.multiple_of(index * slab, slab), slab)

    line = units_line(wire, part, side, row_refs, ti)
    line.lead()
    line.push(0)
    kv_half = w_kv[:, pl.ds(pl.multiple_of(ti * HD, HD), HD)]
    p_in = {}
    for k in (1, 2, 3, 0):
        block = (nt_dot(dq[k], w_q[...]) + nt_dot(dkv[k], kv_half)).astype(BF)
        pbuf[k, 0] = block[0:hrows]
        pbuf[k, 1] = block[hrows : 2 * hrows]
        p_in[k] = wire(pbuf.at[k, other], pside.at[k], "tp", other)
    d_in = {}
    for k in (1, 2, 3, 0):
        p_in[k].wait_recv()
        both = (pbuf[k, ti].astype(F32) + pside[k].astype(F32)).astype(BF)
        if k:
            dbuf[k] = both
            d_in[k] = wire(dbuf.at[k], drow.at[k], "fsdp", fs[k])
        else:
            drow[0] = both
    line.push(1)
    squares = jnp.zeros((hrows, 1), F32)
    for k in range(4):
        u = tok[mine, lanes(fs[k])].astype(F32)
        squares += jnp.sum(u * u, axis=1, keepdims=True)
    r = lax.rsqrt(squares * (1.0 / depth) + 1e-06)
    inner = jnp.zeros((hrows, 1), F32)
    for k in range(4):
        if k:
            d_in[k].wait_recv()
        u = tok[mine, lanes(fs[k])].astype(F32)
        inner += jnp.sum(u * gains_all[k, 0:1, :] * drow[k].astype(F32), axis=1, keepdims=True)
    pull = r * r * r * (inner * (1.0 / depth))
    gpart[...] = gain_part[...]
    for k in range(4):
        at = lanes(fs[k])
        u, d = tok[mine, at].astype(F32), drow[k].astype(F32)
        gbuf[ti, :, at] = d_state[:, at] + (r * (gains_all[k, 0:1, :] * d) - u * pull)
        gpart[k, 0:1, :] = jnp.sum(u * r * d, axis=0, keepdims=True)
    g_side = wire(gbuf.at[ti], gbuf.at[ti], "tp", other)
    g_in = {}
    for k in (1, 2, 3):
        g_in[k] = wire(gpart.at[k], gfar.at[k], "fsdp", fs[k])
    line.push(2)
    line.collect()
    obuf[ti] = (state[...] + line.total[...]).astype(BF)
    o_side = wire(obuf.at[ti], obuf.at[ti], "tp", other)
    total = gpart[0]
    for k in (1, 2, 3):
        g_in[k].wait_recv()
        total += gfar[k]
    for step, (axis, peer) in enumerate((("ctx", cs[1]), ("ctx", cs[2]), ("tp", other))):
        gsum[step] = total
        copy = wire(gsum.at[step], gnear.at[step], axis, peer)
        copy.wait_recv()
        total = total + gnear[step]
    gain_grads[...] = total
    g_side.wait_recv()
    grad_tok[...] = gbuf[...]
    o_side.wait_recv()
    out[...] = obuf[...]
    line.drain()
    wire.finish()


def call_finish(part, state, tok, gains_all, gain_part, d_state, dq, dkv, w_q, w_kv, after):
    hrows, depth = state.shape
    rows, slab = 2 * hrows, depth // 4
    shape = jax.ShapeDtypeStruct
    vmem = pl.BlockSpec(memory_space=pltpu.VMEM)
    hbm = pl.BlockSpec(memory_space=pl.ANY)
    return pl.pallas_call(
        finish_kernel,
        out_shape=[
            shape((2, hrows, depth), BF),
            shape((2, hrows, depth), F32),
            shape((8, slab), F32),
        ],
        in_specs=[vmem] * 10 + [hbm],
        out_specs=[vmem] * 3,
        scratch_shapes=[
            pltpu.VMEM((4, hrows, depth), BF),
            line_scratch(hrows, depth),
            pltpu.VMEM((2, hrows, depth), BF),
            pltpu.VMEM((2, hrows, depth), F32),
            pltpu.VMEM((4, 2, hrows, slab), BF),
            pltpu.VMEM((4, hrows, slab), BF),
            pltpu.VMEM((4, hrows, slab), BF),
            pltpu.VMEM((4, hrows, slab), BF),
            pltpu.VMEM((4, 8, slab), F32),
            pltpu.VMEM((4, 8, slab), F32),
            pltpu.VMEM((3, 8, slab), F32),
            pltpu.VMEM((3, 8, slab), F32),
            pltpu.SemaphoreType.DMA((32,)),
            pltpu.SemaphoreType.DMA((32,)),
        ],
        compiler_params=pltpu.CompilerParams(collective_id=6, has_side_effects=True),
        cost_estimate=pl.CostEstimate(
            flops=2 * 4 * rows * slab * w_q.shape[1], bytes_accessed=150_000_000, transcendentals=0
        ),
        name="finish",
    )(part, state, tok, gains_all, gain_part, d_state, dq, dkv, w_q, w_kv, after)


def fast_device(
    tokens,
    segment_ids,
    w_query,
    w_keyval,
    w_out,
    w_gate,
    w_up,
    w_down,
    gain_attn,
    gain_ffn,
    cotangent,
):
    ci, ti = lax.axis_index("ctx"), lax.axis_index("tp")
    tok, cot = tokens[0], cotangent[0]
    rows, depth = tok.shape
    hrows, slab = rows // 2, depth // 4
    length = segment_ids.shape[1]
    heads = w_query.shape[1] // HD
    units = w_gate.shape[1] // 4

    def cut(value, start, size, axis):
        return lax.dynamic_slice_in_dim(value, start, size, axis)

    segment_row = segment_ids[0]
    local_segment = cut(segment_row, ci * rows, rows, 0)
    local_index = ci * rows + jnp.arange(rows, dtype=jnp.int32)
    earlier = jnp.sum((segment_row[None, :] < local_segment[:, None]).astype(jnp.int32), axis=1)
    position = (local_index - earlier).astype(F32)
    freqs = 10000.0 ** (-(jnp.arange(HD // 4, dtype=F32) * 2.0 / (HD // 2)))
    angle = position[:, None] * freqs[None, :]
    cosine, sine = jnp.cos(angle), jnp.sin(angle)
    cos = jnp.concatenate([cosine, cosine], axis=1)
    sin = jnp.concatenate([-sine, sine], axis=1)
    key_index = jnp.concatenate(
        [(ci ^ k) * rows + jnp.arange(rows, dtype=jnp.int32) for k in range(4)]
    )
    key_segment = jnp.concatenate([cut(segment_row, (ci ^ k) * rows, rows, 0) for k in range(4)])
    keep = (
        (local_segment[:, None] == key_segment[None, :])
        & (key_index[None, :] <= local_index[:, None])
    ).astype(F32)
    gains = jnp.concatenate(
        [gain_attn[None], gain_ffn[None], jnp.zeros((6, slab), gain_attn.dtype)]
    ).astype(F32)

    (
        q_rot,
        kv,
        probs,
        state,
        gains_all,
        normed_all,
        cot_all,
        gate_full,
        up_full,
        normed_slab,
        att_plane,
        gate,
        upward,
        hidden,
        shard_down,
    ) = call_forward(
        heads,
        tok,
        cot,
        gains,
        cos,
        sin,
        keep,
        w_query,
        w_keyval,
        w_out,
        w_gate,
        w_up,
    )
    down_full = call_gather(w_down, shard_down)
    normed_all = normed_all.reshape(length, depth)
    cot_all = cot_all.reshape(length, depth)
    gate_full = gate_full.reshape(depth, units)
    up_full = up_full.reshape(depth, units)
    down_full = down_full.reshape(depth, units)

    grad_down = lax.all_gather(shard_down, "ctx", axis=0, tiled=True)
    d_hidden = matmul(cot_all, down_full)
    _, geglu_pull = jax.vjp(geglu, gate, upward)
    d_gate, d_up = geglu_pull(d_hidden)
    d_gate = d_gate.astype(BF)
    d_up = d_up.astype(BF)
    dn = (times_transposed(d_gate, gate_full) + times_transposed(d_up, up_full)).astype(BF)
    dn = dn.reshape(4, 2, hrows, depth)
    part = times_transposed(hidden, down_full).astype(BF).reshape(4, 2, hrows, depth)
    d_state, gain_part, dq, dkv, weight_grads, gate_all, up_all = call_backward(
        heads,
        dn,
        cot,
        state,
        gains_all,
        probs,
        q_rot,
        kv,
        cos,
        sin,
        w_out,
        normed_slab,
        att_plane,
        normed_all,
        d_gate,
        d_up,
        shard_down,
    )
    weight_grads = lax.all_gather(weight_grads, "ctx", axis=0, tiled=False)
    grad_gate, grad_up, grad_down = call_convert(gate_all, up_all, grad_down)
    out, grad_tok, gain_grads = call_finish(
        part, state, tok, gains_all, gain_part, d_state, dq, dkv, w_query, w_keyval, grad_gate
    )
    quarter = heads * HD // 4
    grad_out = weight_grads[:, 0:quarter].reshape(4 * quarter, slab).astype(F32)
    grad_query = weight_grads[:, quarter : 2 * quarter].reshape(4 * quarter, slab).T.astype(F32)
    kv_mine = weight_grads[:, 2 * quarter :].reshape(HD, slab)
    kv_other = swap(kv_mine, "tp", 2, 1)
    grad_kv = jnp.where(
        ti == 0,
        jnp.concatenate([kv_mine, kv_other], axis=0),
        jnp.concatenate([kv_other, kv_mine], axis=0),
    ).T.astype(F32)

    return (
        out.reshape(1, rows, depth),
        grad_tok.reshape(1, rows, depth),
        grad_query,
        grad_kv,
        grad_out,
        grad_gate,
        grad_up,
        grad_down,
        gain_grads[0],
        gain_grads[1],
    )


def solution(mesh):
    sizes = (mesh.shape["fsdp"], mesh.shape["ctx"], mesh.shape["tp"])
    in_specs = (
        P("fsdp", "ctx", None),
        P("fsdp", None),
        P("fsdp", "tp"),
        P("fsdp", None),
        P("tp", "fsdp"),
        P("fsdp", "tp"),
        P("fsdp", "tp"),
        P("tp", "fsdp"),
        P("fsdp"),
        P("fsdp"),
        P("fsdp", "ctx", None),
    )
    out_specs = (
        P("fsdp", "ctx", None),
        P("fsdp", "ctx", None),
        P("fsdp", "tp"),
        P("fsdp", None),
        P("tp", "fsdp"),
        P("fsdp", "tp"),
        P("fsdp", "tp"),
        P("tp", "fsdp"),
        P("fsdp"),
        P("fsdp"),
    )

    def body(*args):
        rows, depth = args[0].shape[1:]
        fits = sizes == (4, 4, 2) and depth % 512 == 0 and rows % 32 == 0
        if fits:
            return fast_device(*args)
        return per_device(sizes, *args)

    return jax.shard_map(
        body, mesh=mesh, in_specs=in_specs, out_specs=out_specs, check_vma=False
    )
```

profile of v0, /device:TPU:0, one launch (start us, length us, event | category | flops | bytes accessed | tf_op | source)
XLA Modules:
  0.0 802.6 jit_solution(14738245942680889859)
XLA Ops:
  7.2 0.0 all-gather.6.cloned.1.call-start
  7.3 0.7 broadcast_in_dim.7
  8.0 0.7 broadcast_in_dim.6
  8.6 0.7 fusion.9
  9.4 0.9 convert_reduce_fusion
  10.2 0.3 fusion.7
  10.5 0.7 pad_maximum_fusion.cos
  11.3 0.1 pad.18.clone
  11.3 0.7 pad_maximum_fusion.1.sin
  12.1 0.8 and_convert_fusion.keep
  12.9 0.7 maximum_convert_fusion.gains
  13.6 195.1 %attention_forward.1 = (bf16[128,1280]{1,0:T(8,128)(2,1)}, bf16[2,4,128,256]{3,2,1,0:T(8,128)(2,1)}, f32[5,128,512]{2,1,0:T(8,128)}, f32[64,2560]{1,0:T(8,128)},...) custom-call(bf16[128,2560]{1,0:T(8,128)(2,1)} %bitcast.46, ...), custom_call_target="tpu_custom_call" | custom-call | flops 1845493760 | bytes 400000000 | tf_op jit(solution)/shard_map/attention_forward/pallas_call | solution.py:720
  208.7 0.0 copy-start.5
  208.7 0.0 slice-start
  208.7 44.5 %gather_down.1 = bf16[4,640,960]{2,1,0:T(8,128)(2,1)} custom-call(bf16[3840,640]{1,0:T(8,128)(2,1)} %w_down.1, bf16[960,640]{1,0:T(8,128)(2,1)} %get-tuple-element.39.after), custom_call_target="tpu_custom_call" | custom-call | bytes 120000000 | tf_op jit(solution)/shard_map/gather_down/pallas_call | solution.py:427
  253.3 0.0 copy-done.5
  253.3 0.0 copy-start.4
  253.3 0.0 slice-start.1
  253.3 8.2 %multiply_convert_fusion = (bf16[512,960]{1,0:T(8,128)(2,1)S(1)}, bf16[512,960]{1,0:T(8,128)(2,1)S(1)}) fusion(f32[512,960]{1,0:T(8,128)S(1)} %copy-done.5, f32[512,960]{1,0:T(8,128)} %get-tuple-element.43, bf16[512,2560]{1,0:T(8,128)(2,1)} %bitcast.60, bf16[2560,960]{1,0:T(8,128)(2,1)} %bitcast.40), kind=kOutput, calls=%fused_computation.12 | convolution fusion | flops 2528378880 | bytes 13434880 | tf_op jit(solution)/shard_map/dot_general | solution.py:37
  261.5 0.0 copy-start.3
  261.5 0.0 copy-start.2
  261.5 0.0 copy-done.4
  261.5 3.0 fusion.13
  264.5 0.0 copy-done.3
  264.5 4.3 add_convert_fusion
  268.8 282.8 %attention_backward.1 = (f32[64,2560]{1,0:T(8,128)}, f32[4,8,640]{2,1,0:T(8,128)}, bf16[4,128,1280]{2,1,0:T(8,128)(2,1)}, bf16[4,128,256]{2,1,0:T(8,128)(2,1)}, ...) custom-call(bf16[4,2,64,2560]{3,2,1,0:T(8,128)(2,1)} %bitcast.50, ...), custom_call_target="tpu_custom_call" | custom-call | flops 838860800 | bytes 300000000 | tf_op jit(solution)/shard_map/attention_backward/pallas_call | solution.py:1262
  551.7 0.0 all-gather.6.cloned.1.call-update
  551.7 0.3 all-gather.4.cloned.1.call-start
  552.0 0.5 all-gather.4.cloned.1.call-update
  552.5 0.4 copy-done.6
  552.9 6.7 convolution_convert_fusion
  559.7 60.8 %all-gather.6.cloned.1.call-done = bf16[2816,640]{1,0:T(8,128)(2,1)} async-done(((bf16[704,640]{1,0:T(8,128)(2,1)}), bf16[2816,640]{1,0:T(8,128)(2,1)}) %all-gather.6.cloned.1.call-update) | async-done | bytes 3604496 | tf_op jit(solution)/shard_map/all_gather | solution.py:1661
  620.5 1.7 slice.21
  622.2 3.4 fusion.12
  625.6 0.4 convert_bitcast_fusion
  625.9 3.0 copy.27
  628.9 0.0 collective-permute-start
  628.9 3.5 bitcast_convert_fusion
  632.4 0.0 collective-permute-done
  632.4 0.2 convert_bitcast_fusion.1
  632.6 1.5 copy.28
  634.1 79.2 %all-gather.4.cloned.1.call-done.down_all = bf16[3840,640]{1,0:T(8,128)(2,1)} async-done(((bf16[960,640]{1,0:T(8,128)(2,1)}), bf16[3840,640]{1,0:T(8,128)(2,1)}) %all-gather.4.cloned.1.call-update) | async-done | bytes 4915216 | tf_op jit(solution)/shard_map/all_gather | solution.py:1633
  713.3 20.8 %convert.18 = (f32[640,3840]{1,0:T(8,128)}, f32[640,3840]{1,0:T(8,128)}, f32[3840,640]{1,0:T(8,128)}) custom-call(bf16[4,640,960]{2,1,0:T(8,128)(2,1)} %get-tuple-element.57.gate_all, bf16[4,640,960]{2,1,0:T(8,128)(2,1)} %get-tuple-element.58.up_all, bf16[3840,640]{1,0:T(8,128)(2,1)} %all-gather.4.cloned.1.call-done.down_all), custom_call_target="tpu_custom_call" | custom-call | bytes 44236800 | tf_op jit(solution)/shard_map/convert/pallas_call | solution.py:1378
  734.1 56.9 %finish.1 = (bf16[2,64,2560]{2,1,0:T(8,128)(2,1)}, f32[2,64,2560]{2,1,0:T(8,128)}, f32[8,640]{1,0:T(8,128)}) custom-call(bf16[4,2,64,2560]{3,2,1,0:T(8,128)(2,1)} %bitcast.48, f32[64,2560]{1,0:T(8,128)} %get-tuple-element.40.state, bf16[128,2560]{1,0:T(8,128)(2,1)} %bitcast.47, f32[4,8,640]{2,1,0:T(8,128)} %get-tuple-element.41.gains_all, ...), custom_call_target="tpu_custom_call" | custom-call | flops 838860800 | bytes 150000000 | tf_op jit(solution)/shard_map/finish/pallas_call | solution.py:1517
  791.0 0.0 copy-start
  791.0 1.5 slice_reduce_fusion
  792.5 2.0 copy.32
  794.4 1.1 copy.33
  (15 shorter events, 0.1 us)
Async XLA Ops:
  7.2 613.3 %all-gather.6.cloned.1.call-start = ((), (), s32[]{:S(2)}) async-start(), calls=%async_computation.1 | async-start | bytes 4505600 | tf_op jit(solution)/shard_map/all_gather | solution.py:1661
  208.7 44.6 %copy-start.5 = (f32[512,960]{1,0:T(8,128)S(1)}, f32[512,960]{1,0:T(8,128)}, u32[]{:S(2)}) copy-start(f32[512,960]{1,0:T(8,128)} %get-tuple-element.44) | copy-start | bytes 5898244
  208.7 55.8 %slice-start = ((s8[5242880]{0:T(1024)(128)(4,1)}), s8[1048576]{0:T(1024)(128)(4,1)S(1)}, s32[]{:S(2)}) async-start(s8[5242880]{0:T(1024)(128)(4,1)} %bitcast.56), calls=%async_computation.2 | async-start | bytes 2097152
  253.3 8.2 %copy-start.4 = (bf16[4,640,960]{2,1,0:T(8,128)(2,1)S(1)}, bf16[4,640,960]{2,1,0:T(8,128)(2,1)}, u32[]{:S(2)}) copy-start(bf16[4,640,960]{2,1,0:T(8,128)(2,1)} %get-tuple-element.45) | copy-start | bytes 14745604
  253.3 11.2 %slice-start.1 = ((s8[5242880]{0:T(1024)(128)(4,1)}), s8[4194304]{0:T(1024)(128)(4,1)S(1)}, s32[]{:S(2)}) async-start(s8[5242880]{0:T(1024)(128)(4,1)} %bitcast.56), calls=%async_computation.3 | async-start | bytes 8388608
  261.5 3.0 copy-start.3
  261.5 3.0 copy-start.2
  551.7 1.2 copy-start.6
  551.7 161.5 %all-gather.4.cloned.1.call-start = ((), (), s32[]{:S(2)}) async-start(), calls=%async_computation | async-start | bytes 6144000 | tf_op jit(solution)/shard_map/all_gather | solution.py:1633
  628.9 3.5 collective-permute-start
  628.9 3.5 copy-start.1
  791.0 3.4 copy-start
Sparse Core Ops, SparseCore 0:
  551.9 68.5 all-gather.5
  622.0 91.1 all-gather.3
where the time goes:
time: 809 us; the launch traced here: 803 us
  Pallas kernels  600 us (74%)
  waiting for transfers between devices  141 us (17%)
  matrix products  22.2 us (3%)
  local copies, waits for them, and re-layouts  16.6 us (2%)
  between operations  14.5 us (2%)
  other arithmetic  8.18 us (1%)
    pallas_call x1, Pallas kernels, call_backward(): pl.pallas_call(functools.partial(backward_kernel, heads), out_shape=[shap...  283 us
    pallas_call x1, Pallas kernels, call_forward(): pl.pallas_call(functools.partial(forward_kernel, heads), out_shape=[shape...  195 us
    all_gather x1, waiting for transfers between devices, fast_device(): grad_down = lax.all_gather(shard_down, 'ctx', axis=0, tiled=True)  79.2 us
    all_gather x1, waiting for transfers between devices, fast_device(): weight_grads = lax.all_gather(weight_grads, 'ctx', axis=0, tiled=False)  60.8 us
    pallas_call x1, Pallas kernels, call_finish(): pl.pallas_call(finish_kernel, out_shape=[shape((2, hrows, depth), BF), sh...  56.9 us
    pallas_call x1, Pallas kernels, call_gather(): pl.pallas_call(gather_kernel, out_shape=jax.ShapeDtypeStruct((4, slab, un...  44.5 us
    pallas_call x1, Pallas kernels, call_convert(): pl.pallas_call(convert_kernel, out_shape=[shape((slab, 4 * units), F32),...  20.8 us
  transfers between devices with their start and end apart: 3, of which 2 were waited for; matrix products, arithmetic and copies ran while one was open for 3% of the time, Pallas kernels for 0%

commit v1 on v0

--- a/solution.py
+++ b/solution.py
@@ -6,7 +6,6 @@
 from jax.experimental import pallas as pl
 from jax.experimental.pallas import tpu as pltpu
 from jax.sharding import PartitionSpec as P
-
 
 HD = 256
 NEGATIVE = -1e30
@@ -393,53 +392,167 @@
             copy.wait_recv()
 
 
-def gather_kernel(w_down, after, down_full, down_rows, own, send, recv, local):
-    del after
-    fs = partners("fsdp", 4)
+def middle_kernel(
+    w_down,
+    shard_down,
+    cot_in,
+    normed_in,
+    gate_in,
+    up_in,
+    hidden_in,
+    gate_w_in,
+    up_w_in,
+    d_up,
+    dn,
+    part,
+    shard_gate,
+    down_all,
+    down_rows,
+    dfull,
+    cot,
+    normed,
+    gate,
+    upward,
+    hidden,
+    gate_w,
+    up_w,
+    dh,
+    d_gate,
+    parts,
+    near,
+    far,
+    sums,
+    sems,
+    send,
+    recv,
+    local,
+):
+    fs, cs = partners("fsdp", 4), partners("ctx", 4)
     ci = lax.axis_index("ctx")
     units, slab = down_rows.shape
-    load = pltpu.make_async_copy(
-        w_down.at[pl.ds(pl.multiple_of(ci * units, 64), units), :], down_rows, local.at[0]
-    )
-    load.start()
-    greet([("fsdp", fs[1]), ("fsdp", fs[2])])
+    length, _ = cot.shape
+    loads = [
+        pltpu.make_async_copy(source, target, local.at[n])
+        for n, (source, target) in enumerate(
+            (
+                (w_down.at[pl.ds(pl.multiple_of(ci * units, 64), units), :], down_rows),
+                (cot_in, cot),
+                (gate_in, gate),
+                (up_in, upward),
+                (normed_in, normed),
+                (gate_w_in, gate_w),
+                (up_w_in, up_w),
+                (hidden_in, hidden),
+            )
+        )
+    ]
+    loads[0].start()
+    greet([("fsdp", fs[1]), ("fsdp", fs[2]), ("ctx", cs[1]), ("ctx", cs[3])])
+    for load in loads[1:]:
+        load.start()
     wire = Wire(send, recv)
-    gather = Gather(
-        wire, fs, 8, slab // 8, lambda m, index, at: down_full.at[index, at, :], own=own
-    )
-    keep = pltpu.make_async_copy(own, down_full.at[fs[0]], local.at[1])
+    spread = Spread(shard_down, down_all, PIECES, *sems)
+    spread.begin()
+    for p in range(PIECES):
+        spread.give(p)
+    gather = Gather(wire, fs, 8, slab // 8, lambda m, index, at: dfull.at[index, at, :])
 
     def prepare(m):
+        loads[0].wait()
+        dfull[fs[0]] = down_rows[...].T
+
+    def lanes(index):
+        return pl.ds(pl.multiple_of(index * slab, slab), slab)
+
+    for n, _ in enumerate(gather.steps((0,), prepare)):
+        if n == 3:
+            loads[1].wait()
+            dh[...] = jnp.dot(cot[:, lanes(fs[0])], dfull[fs[0]], preferred_element_type=F32)
+        if n >= 8:
+            spread.hand_on(n - 8)
+    for load in loads[2:]:
         load.wait()
-        own[...] = down_rows[...].T
-        keep.start()
-
-    for _ in gather.steps((0,), prepare):
-        pass
     gather.settle()
-    keep.wait()
+    for k in (1, 2, 3):
+        dh[...] += jnp.dot(cot[:, lanes(fs[k])], dfull[fs[k]], preferred_element_type=F32)
+    step = 128
+    for n in range(length // step):
+        at = slice(n * step, (n + 1) * step)
+        v, d = gate[at, :], dh[at, :]
+        square = v * v
+        t = jnp.tanh(0.7978845608028654 * (v + 0.044715 * (square * v)))
+        cdf = 0.5 * (1.0 + t)
+        slope = cdf + (0.5 * v) * (1.0 - t * t) * (
+            0.7978845608028654 * (1.0 + 0.134145 * square)
+        )
+        d_gate[at, :] = (d * upward[at, :] * slope).astype(BF)
+        d_up[at, :] = (d * (v * cdf)).astype(BF)
+    product = Product(wire, False, normed, d_gate, shard_gate, parts, near, far, sums)
+    product.start()
+    for p in range(PIECES // 2):
+        spread.hand_far(p)
+    for j in range(4):
+        block = nt_dot(d_gate[...], gate_w[j]) + nt_dot(d_up[...], up_w[j])
+        dn[:, j * slab : (j + 1) * slab] = block.astype(BF)
+    product.middle()
+    for p in range(PIECES // 2, PIECES):
+        spread.hand_far(p)
+    for j in range(4):
+        part[:, j * slab : (j + 1) * slab] = nt_dot(hidden[...], dfull[j]).astype(BF)
+    product.end()
+    spread.close()
     wire.finish()
 
 
-def call_gather(w_down, after):
-    units, slab = w_down.shape[0] // 4, w_down.shape[1]
+def call_middle(w_down, shard_down, cot, normed, gate, upward, hidden, gate_w, up_w):
+    units, slab = shard_down.shape
+    length, depth = cot.shape
+    sizes = product_sizes(False, slab, units)
+    pair = [pltpu.VMEM((2, *size), BF) for size in sizes]
+    single = [pltpu.VMEM(size, BF) for size in sizes]
+    shape = jax.ShapeDtypeStruct
+    vmem = pl.BlockSpec(memory_space=pltpu.VMEM)
     hbm = pl.BlockSpec(memory_space=pl.ANY)
     return pl.pallas_call(
-        gather_kernel,
-        out_shape=jax.ShapeDtypeStruct((4, slab, units), BF),
-        in_specs=[hbm] * 2,
-        out_specs=hbm,
+        middle_kernel,
+        out_shape=[
+            shape((length, units), BF),
+            shape((length, depth), BF),
+            shape((length, depth), BF),
+            shape((slab, units), BF),
+            shape((4, units, slab), BF),
+        ],
+        in_specs=[hbm] * 9,
+        out_specs=[vmem] * 4 + [hbm],
         scratch_shapes=[
             pltpu.VMEM((units, slab), BF),
-            pltpu.VMEM((slab, units), BF),
-            pltpu.SemaphoreType.DMA((24,)),
-            pltpu.SemaphoreType.DMA((24,)),
-            pltpu.SemaphoreType.DMA((2,)),
+            pltpu.VMEM((4, slab, units), BF),
+            pltpu.VMEM((length, depth), BF),
+            pltpu.VMEM((length, depth), BF),
+            pltpu.VMEM((length, units), F32),
+            pltpu.VMEM((length, units), F32),
+            pltpu.VMEM((length, units), BF),
+            pltpu.VMEM((4, slab, units), BF),
+            pltpu.VMEM((4, slab, units), BF),
+            pltpu.VMEM((length, units), F32),
+            pltpu.VMEM((length, units), BF),
+            list(pair),
+            list(pair),
+            list(single),
+            list(single),
+            spread_scratch(PIECES),
+            pltpu.SemaphoreType.DMA((32,)),
+            pltpu.SemaphoreType.DMA((32,)),
+            pltpu.SemaphoreType.DMA((8,)),
         ],
-        compiler_params=pltpu.CompilerParams(collective_id=2, has_side_effects=True),
-        cost_estimate=pl.CostEstimate(flops=0, bytes_accessed=120_000_000, transcendentals=0),
-        name="gather_down",
-    )(w_down, after)
+        compiler_params=pltpu.CompilerParams(
+            collective_id=2, has_side_effects=True, vmem_limit_bytes=67_043_328
+        ),
+        cost_estimate=pl.CostEstimate(
+            flops=12 * length * depth * units, bytes_accessed=300_000_000, transcendentals=0
+        ),
+        name="feed_forward_backward",
+    )(w_down, shard_down, cot, normed, gate, upward, hidden, gate_w, up_w)
 
 
 def forward_kernel(
@@ -873,17 +986,31 @@
                     self.outbox[way, u - 1 + way] = self.own(u).astype(BF)
                     self.copy(way, u).start()
 
-    def push(self, step):
-        for way, u in ((0, 3 - step), (1, step)):
-
-            @pl.when(jnp.logical_and(self.sends(way, u), self.fed(way)))
-            def _():
-                self.copy(way, u).wait_recv()
-                slot = u - 1 + way
-                self.outbox[way, slot] = (
-                    self.own(u) + self.inbox[way, slot].astype(F32)
-                ).astype(BF)
-                self.copy(way, u).start()
+    def hop(self, way, u):
+        self.copy(way, u).wait_recv()
+        slot = u - 1 + way
+        self.outbox[way, slot] = (self.own(u) + self.inbox[way, slot].astype(F32)).astype(BF)
+        self.copy(way, u).start()
+
+    def push_near(self):
+        @pl.when(self.ci == 1)
+        def _():
+            self.hop(0, 3)
+            self.hop(0, 2)
+
+        @pl.when(self.ci == 2)
+        def _():
+            self.hop(1, 0)
+            self.hop(1, 1)
+
+    def push_far(self):
+        @pl.when(self.ci == 1)
+        def _():
+            self.hop(1, 0)
+
+        @pl.when(self.ci == 2)
+        def _():
+            self.hop(0, 3)
 
     def collect(self):
         self.total[...] = self.own(self.ci)
@@ -914,14 +1041,14 @@
 
 
 class Spread:
-    def __init__(self, own, full, pieces, send, recv, local):
+    def __init__(self, own, full, pieces, send, recv, local, height=None):
         self.own, self.full, self.pieces = own, full, pieces
         self.send, self.recv = send, recv
-        self.height = own.shape[0] // pieces
+        self.height = height or own.shape[0] // pieces
         self.cs = partners("ctx", 4)
         self.ci = self.cs[0]
         self.inner = jnp.logical_and(self.ci > 0, self.ci < 3)
-        self.local = pltpu.make_async_copy(own, full.at[self.ci], local)
+        self.local = local
 
     def strip(self, p):
         return pl.ds(p * self.height, self.height)
@@ -948,8 +1075,11 @@
     def arrived(self, slot, p):
         self.copy((0, 1, 2)[slot], p, self.ci, self.cs[1]).wait_recv()
 
+    def keep(self):
+        return pltpu.make_async_copy(self.own, self.full.at[self.ci], self.local)
+
     def begin(self):
-        self.local.start()
+        self.keep().start()
 
     def give(self, p):
         self.out(0, p).start()
@@ -972,22 +1102,31 @@
             self.arrived(2, p)
             self.out(4, p).start()
 
-    def close(self):
+    def close(self, near=True, far=True):
         for p in range(self.pieces):
 
             @pl.when(jnp.logical_not(self.inner))
             def _():
-                for slot in range(3):
+                for slot in range(0 if near else 2, 3 if far else 2):
                     self.arrived(slot, p)
 
-            self.out(0, p).wait_send()
+            if near:
+                self.out(0, p).wait_send()
 
             @pl.when(self.inner)
             def _():
-                for kind in range(1, 5):
+                if near and not far:
+                    self.arrived(2, p)
+                for kind in range(1 if near else 4, 5 if far else 4):
                     self.out(kind, p).wait_send()
 
-        self.local.wait()
+        if near:
+            self.keep().wait()
+
+    def hand_again(self, p):
+        @pl.when(self.inner)
+        def _():
+            self.out(4, p).start()
 
 
 def spread_scratch(pieces):
@@ -1021,16 +1160,18 @@
     normed,
     att,
     normed_all,
-    d_gate,
+    shard_gate,
     d_up,
-    after,
-    d_state,
-    gain_part,
-    dq_plane,
-    dkv_plane,
-    weight_grads,
+    part,
+    tok,
+    w_q,
+    w_kv,
+    out,
+    grad_tok,
+    gain_grads,
     gate_all,
     up_all,
+    weights_all,
     side,
     dbuf,
     dslab,
@@ -1051,19 +1192,30 @@
     query_refs,
     parts,
     sums,
-    gate_recv,
-    up_recv,
-    shard_gate,
+    product_recv,
     shard_up,
     gate_sems,
     up_sems,
+    gpart,
+    weight_grads,
+    weight_sems,
+    last_sems,
+    obuf,
+    gbuf,
+    pbuf,
+    pside,
+    nbuf,
+    nrow,
+    gfar,
+    gsum,
+    gnear,
+    gall,
     send,
     recv,
     local,
 ):
-    del after
     fs, cs = partners("fsdp", 4), partners("ctx", 4)
-    ti = lax.axis_index("tp")
+    ci, ti = lax.axis_index("ctx"), lax.axis_index("tp")
     other = 1 - ti
     hrows, depth = state.shape
     rows = 2 * hrows
@@ -1081,26 +1233,25 @@
     def lanes(index):
         return pl.ds(pl.multiple_of(index * slab, slab), slab)
 
-    gate = Product(wire, False, normed_all, d_gate, shard_gate, parts, *gate_recv, sums)
-    up = Product(wire, False, normed_all, d_up, shard_up, parts, *up_recv, sums)
+    up = Product(wire, False, normed_all, d_up, shard_up, parts, *product_recv, sums)
     gate_line = Spread(shard_gate, gate_all, PIECES, *gate_sems)
     up_line = Spread(shard_up, up_all, PIECES, *up_sems)
-    gate.start()
     line = units_line(wire, dn, side, row_refs, ti)
     line.lead()
+    gate_line.begin()
+    for p in range(PIECES // 2):
+        gate_line.give(p)
+    up.start()
     squares = jnp.zeros((hrows, 1), F32)
     for k in range(4):
         u = state[:, lanes(fs[k])]
         squares += jnp.sum(u * u, axis=1, keepdims=True)
     r = lax.rsqrt(squares * (1.0 / depth) + 1e-06)
-    gate.middle()
-    line.push(0)
-    line.push(1)
-    gate.end()
-    gate_line.begin()
-    for p in range(PIECES):
+    line.push_near()
+    line.push_far()
+    for p in range(PIECES // 2, PIECES):
         gate_line.give(p)
-    line.push(2)
+    up.middle()
     line.collect()
     inner = jnp.zeros((hrows, 1), F32)
     for k in range(4):
@@ -1111,22 +1262,24 @@
     pull = r * r * r * (inner * (1.0 / depth))
     d_in = {}
     d_side = {}
-    gain_part[...] = jnp.zeros_like(gain_part)
+    gpart[...] = jnp.zeros_like(gpart)
     for k in (1, 2, 3, 0):
         at = lanes(fs[k])
         u, d = state[:, at], line.total[:, at]
         ds = cot[mine, at].astype(F32) + (r * (gains_all[k, 1:2, :] * d) - u * pull)
-        d_state[:, at] = ds
+        gbuf[ti, :, at] = ds
         if k:
             dbuf[k] = ds.astype(BF)
             d_in[k] = wire(dbuf.at[k], dslab.at[k, ti], "fsdp", fs[k])
         else:
             dslab[0, ti] = ds.astype(BF)
             d_side[0] = wire(dslab.at[0, ti], dslab.at[0, ti], "tp", other)
-        gain_part[k, 1:2, :] = jnp.sum(u * r * d, axis=0, keepdims=True)
+        gpart[k, 1:2, :] = jnp.sum(u * r * d, axis=0, keepdims=True)
     for k in (1, 2, 3):
         d_in[k].wait_recv()
         d_side[k] = wire(dslab.at[k, ti], dslab.at[k, ti], "tp", other)
+    for p in range(PIECES // 2):
+        gate_line.hand_on(p)
     a_in = {}
     for k in (1, 2, 3, 0):
         d_side[k].wait_recv()
@@ -1134,8 +1287,9 @@
         dpart[k] = nt_dot(block, w_o[...]).astype(BF)
         if k:
             a_in[k] = wire(dpart.at[k], dfar.at[k], "fsdp", fs[k])
-    wire.settle(list(gate.one.values()) + list(gate.two.values()))
-    up.start()
+    for p in range(PIECES // 2, PIECES):
+        gate_line.hand_on(p)
+    up.end()
     keys = kv[0].reshape(length, HD)
     values = kv[1].reshape(length, HD)
     c, s = cos[...], sin[...]
@@ -1167,6 +1321,8 @@
         else:
             dk_acc[...] += dk
             dv_acc[...] += dv
+    for p in range(PIECES // 2):
+        gate_line.hand_far(p)
     dkv2[0] = (dk_acc[...] * scale).astype(BF).reshape(4, rows, HD)
     dkv2[1] = dv_acc[...].astype(BF).reshape(4, rows, HD)
     k_side = wire(dkv2.at[other], kvt, "tp", other)
@@ -1178,9 +1334,9 @@
     for k in (1, 2, 3):
         zk[k] = (dkv2[ti, k].astype(F32) + kvt[k].astype(F32)).astype(BF)
         z_in[k] = wire(zk.at[k], zfar.at[k], "ctx", cs[k])
-    for p in range(PIECES // 2):
-        gate_line.hand_on(p)
     out_line.lead()
+    for p in range(PIECES // 2, PIECES):
+        gate_line.hand_far(p)
     own = dkv2[ti, 0].astype(F32) + kvt[0].astype(F32)
     for k in (1, 2, 3):
         z_in[k].wait_recv()
@@ -1190,10 +1346,10 @@
     v_in = {}
     for k in (1, 2, 3):
         v_in[k] = wire(dkvbuf.at[0], dkvbuf.at[k], "fsdp", fs[k])
-    up.middle()
-    for p in range(PIECES // 2, PIECES):
-        gate_line.hand_on(p)
-    out_line.push(0)
+    up_line.begin()
+    for p in range(PIECES):
+        up_line.give(p)
+    out_line.push_near()
     for k in (1, 2, 3):
         q_in[k].wait_recv()
     slabs = normed[...].reshape(length, slab)
@@ -1202,44 +1358,104 @@
         own_query[u, 0:quarter] = tn_dot(columns, slabs).astype(BF)
     for k in (1, 2, 3):
         v_in[k].wait_recv()
-    keep_q = pltpu.make_async_copy(dqbuf, dq_plane, local.at[0])
-    keep_v = pltpu.make_async_copy(dkvbuf, dkv_plane, local.at[1])
-    keep_q.start()
-    keep_v.start()
     for u in (3, 0, 2, 1):
         columns = dkvbuf[:, :, u * (HD // 4) : (u + 1) * (HD // 4)].reshape(length, HD // 4)
         own_query[u, quarter:] = tn_dot(columns, slabs).astype(BF)
     query_line = Line(lambda u: own_query[u].astype(F32), *query_refs)
+    kv_half = w_kv[:, pl.ds(pl.multiple_of(ti * HD, HD), HD)]
+    p_in = {}
+    for k in (1, 2, 3, 0):
+        block = (nt_dot(dqbuf[k], w_q[...]) + nt_dot(dkvbuf[k], kv_half)).astype(BF)
+        pbuf[k, 0] = block[0:hrows]
+        pbuf[k, 1] = block[hrows:rows]
+        p_in[k] = wire(pbuf.at[k, other], pside.at[k], "tp", other)
+    out_line.push_far()
     query_line.lead()
-    for p in range(PIECES // 2):
-        gate_line.hand_far(p)
-    up.end()
-    up_line.begin()
-    for p in range(PIECES // 2):
-        up_line.give(p)
-    out_line.push(1)
-    query_line.push(0)
-    for p in range(PIECES // 2, PIECES):
-        gate_line.hand_far(p)
-    for p in range(PIECES // 2, PIECES):
-        up_line.give(p)
-    out_line.push(2)
-    query_line.push(1)
-    query_line.push(2)
+    n_in = {}
+    for k in (1, 2, 3, 0):
+        p_in[k].wait_recv()
+        both = (pbuf[k, ti].astype(F32) + pside[k].astype(F32)).astype(BF)
+        if k:
+            nbuf[k] = both
+            n_in[k] = wire(nbuf.at[k], nrow.at[k], "fsdp", fs[k])
+        else:
+            nrow[0] = both
+    squares = jnp.zeros((hrows, 1), F32)
+    for k in range(4):
+        u = tok[mine, lanes(fs[k])].astype(F32)
+        squares += jnp.sum(u * u, axis=1, keepdims=True)
+    r = lax.rsqrt(squares * (1.0 / depth) + 1e-06)
     for p in range(PIECES):
         up_line.hand_on(p)
+    line.drain()
+    last = units_line(wire, part, side, [*row_refs[:3], *last_sems], ti)
+    last.lead()
+    for p in range(PIECES // 2):
+        up_line.hand_far(p)
+    inner = jnp.zeros((hrows, 1), F32)
+    for k in range(4):
+        if k:
+            n_in[k].wait_recv()
+        u = tok[mine, lanes(fs[k])].astype(F32)
+        inner += jnp.sum(u * gains_all[k, 0:1, :] * nrow[k].astype(F32), axis=1, keepdims=True)
+    pull = r * r * r * (inner * (1.0 / depth))
+    for k in range(4):
+        at = lanes(fs[k])
+        u, d = tok[mine, at].astype(F32), nrow[k].astype(F32)
+        gbuf[ti, :, at] += (r * (gains_all[k, 0:1, :] * d) - u * pull)
+        gpart[k, 0:1, :] = jnp.sum(u * r * d, axis=0, keepdims=True)
+    t_side = wire(gbuf.at[ti], gbuf.at[ti], "tp", other)
+    g_in = {}
+    for k in (1, 2, 3):
+        g_in[k] = wire(gpart.at[k], gfar.at[k], "fsdp", fs[k])
+    for p in range(PIECES // 2, PIECES):
+        up_line.hand_far(p)
+    query_line.push_near()
+    gain_sum = gpart[0]
+    for k in (1, 2, 3):
+        g_in[k].wait_recv()
+        gain_sum += gfar[k]
+    gsum[...] = gain_sum
+    near_gain = wire(gsum, gnear, "tp", other)
+    near_gain.wait_recv()
+    gall[ci] = gain_sum + gnear[...]
+    all_gain = [wire(gall.at[ci], gall.at[ci], "ctx", cs[k]) for k in (1, 2, 3)]
+    query_line.push_far()
+    last.push_near()
     out_line.collect()
     weight_grads[0:quarter, :] = out_line.total[...].astype(BF)
     query_line.collect()
     weight_grads[quarter:, :] = query_line.total[...].astype(BF)
+    weight_line = Spread(weight_grads, weights_all, PIECES, *weight_sems)
+    weight_line.begin()
     for p in range(PIECES):
-        up_line.hand_far(p)
+        weight_line.give(p)
+    last.push_far()
+    for p in range(PIECES):
+        weight_line.hand_on(p)
+    for p in range(PIECES // 2):
+        weight_line.hand_far(p)
+    last.collect()
+    obuf[ti] = (state[...] + last.total[...]).astype(BF)
+    o_side = wire(obuf.at[ti], obuf.at[ti], "tp", other)
+    for p in range(PIECES // 2, PIECES):
+        weight_line.hand_far(p)
+    t_side.wait_recv()
+    keep_t = pltpu.make_async_copy(gbuf, grad_tok, local.at[0])
+    keep_t.start()
+    o_side.wait_recv()
+    keep_o = pltpu.make_async_copy(obuf, out, local.at[1])
+    keep_o.start()
+    for copy in all_gain:
+        copy.wait_recv()
+    gain_grads[...] = gall[0] + gall[1] + gall[2] + gall[3]
     gate_line.close()
     up_line.close()
-    for each in (line, out_line, query_line):
+    weight_line.close()
+    for each in (last, out_line, query_line):
         each.drain()
-    keep_q.wait()
-    keep_v.wait()
+    keep_t.wait()
+    keep_o.wait()
     wire.finish()
 
 
@@ -1247,12 +1463,12 @@
 
 
 def call_backward(
-    heads, dn, cot, state, gains_all, probs, q_rot, kv, cos, sin, w_o, normed, att, normed_all, d_gate, d_up, after
+    heads, dn, cot, state, gains_all, probs, q_rot, kv, cos, sin, w_o, normed, att, normed_all, shard_gate, d_up, part, tok, w_q, w_kv
 ):
     hrows, depth = state.shape
     rows, slab, qcols = 2 * hrows, depth // 4, heads * HD
     length = 4 * rows
-    units = d_gate.shape[1]
+    units = d_up.shape[1]
     sizes = product_sizes(False, slab, units)
     pair = [pltpu.VMEM((2, *size), BF) for size in sizes]
     single = [pltpu.VMEM(size, BF) for size in sizes]
@@ -1262,16 +1478,15 @@
     return pl.pallas_call(
         functools.partial(backward_kernel, heads),
         out_shape=[
-            shape((hrows, depth), F32),
-            shape((4, 8, slab), F32),
-            shape((4, rows, qcols), BF),
-            shape((4, rows, HD), BF),
-            shape((qcols // 2 + HD // 4, slab), BF),
+            shape((2, hrows, depth), BF),
+            shape((2, hrows, depth), F32),
+            shape((8, slab), F32),
             shape((4, slab, units), BF),
             shape((4, slab, units), BF),
+            shape((4, qcols // 2 + HD // 4, slab), BF),
         ],
-        in_specs=[vmem] * 15 + [hbm],
-        out_specs=[vmem] * 2 + [hbm] * 2 + [vmem] + [hbm] * 2,
+        in_specs=[vmem] * 13 + [hbm] + [vmem] * 5,
+        out_specs=[hbm] * 2 + [vmem] + [hbm] * 3,
         scratch_shapes=[
             pltpu.VMEM((4, hrows, depth), BF),
             pltpu.VMEM((4, hrows, slab), BF),
@@ -1294,13 +1509,25 @@
             list(pair),
             list(single),
             [list(pair), list(single)],
-            [list(pair), list(single)],
-            pltpu.VMEM((slab, units), BF),
             pltpu.VMEM((slab, units), BF),
             spread_scratch(PIECES),
             spread_scratch(PIECES),
-            pltpu.SemaphoreType.DMA((48,)),
-            pltpu.SemaphoreType.DMA((48,)),
+            pltpu.VMEM((4, 8, slab), F32),
+            pltpu.VMEM((qcols // 2 + HD // 4, slab), BF),
+            spread_scratch(PIECES),
+            [pltpu.SemaphoreType.DMA((2, 3)), pltpu.SemaphoreType.DMA((2, 3))],
+            pltpu.VMEM((2, hrows, depth), BF),
+            pltpu.VMEM((2, hrows, depth), F32),
+            pltpu.VMEM((4, 2, hrows, slab), BF),
+            pltpu.VMEM((4, hrows, slab), BF),
+            pltpu.VMEM((4, hrows, slab), BF),
+            pltpu.VMEM((4, hrows, slab), BF),
+            pltpu.VMEM((4, 8, slab), F32),
+            pltpu.VMEM((8, slab), F32),
+            pltpu.VMEM((8, slab), F32),
+            pltpu.VMEM((4, 8, slab), F32),
+            pltpu.SemaphoreType.DMA((64,)),
+            pltpu.SemaphoreType.DMA((64,)),
             pltpu.SemaphoreType.DMA((2,)),
         ],
         compiler_params=pltpu.CompilerParams(
@@ -1310,7 +1537,7 @@
             flops=2 * length * slab * qcols, bytes_accessed=300_000_000, transcendentals=0
         ),
         name="attention_backward",
-    )(dn, cot, state, gains_all, probs, q_rot, kv, cos, sin, w_o, normed, att, normed_all, d_gate, d_up, after)
+    )(dn, cot, state, gains_all, probs, q_rot, kv, cos, sin, w_o, normed, att, normed_all, shard_gate, d_up, part, tok, w_q, w_kv)
 
 
 STRIP = 80
@@ -1395,156 +1622,6 @@
         ),
         name="convert",
     )(gate_all, up_all, down_all)
-
-
-def finish_kernel(
-    part,
-    state,
-    tok,
-    gains_all,
-    gain_part,
-    d_state,
-    dq,
-    dkv,
-    w_q,
-    w_kv,
-    after,
-    out,
-    grad_tok,
-    gain_grads,
-    side,
-    row_refs,
-    obuf,
-    gbuf,
-    pbuf,
-    pside,
-    dbuf,
-    drow,
-    gpart,
-    gfar,
-    gsum,
-    gnear,
-    send,
-    recv,
-):
-    del after
-    fs, cs = partners("fsdp", 4), partners("ctx", 4)
-    ti = lax.axis_index("tp")
-    other = 1 - ti
-    hrows, depth = state.shape
-    slab = depth // 4
-    greet(
-        [("fsdp", fs[k]) for k in (1, 2, 3)]
-        + [("ctx", cs[k]) for k in (1, 2, 3)]
-        + [("tp", other)]
-    )
-    wire = Wire(send, recv)
-    mine = pl.ds(pl.multiple_of(ti * hrows, hrows), hrows)
-
-    def lanes(index):
-        return pl.ds(pl.multiple_of(index * slab, slab), slab)
-
-    line = units_line(wire, part, side, row_refs, ti)
-    line.lead()
-    line.push(0)
-    kv_half = w_kv[:, pl.ds(pl.multiple_of(ti * HD, HD), HD)]
-    p_in = {}
-    for k in (1, 2, 3, 0):
-        block = (nt_dot(dq[k], w_q[...]) + nt_dot(dkv[k], kv_half)).astype(BF)
-        pbuf[k, 0] = block[0:hrows]
-        pbuf[k, 1] = block[hrows : 2 * hrows]
-        p_in[k] = wire(pbuf.at[k, other], pside.at[k], "tp", other)
-    d_in = {}
-    for k in (1, 2, 3, 0):
-        p_in[k].wait_recv()
-        both = (pbuf[k, ti].astype(F32) + pside[k].astype(F32)).astype(BF)
-        if k:
-            dbuf[k] = both
-            d_in[k] = wire(dbuf.at[k], drow.at[k], "fsdp", fs[k])
-        else:
-            drow[0] = both
-    line.push(1)
-    squares = jnp.zeros((hrows, 1), F32)
-    for k in range(4):
-        u = tok[mine, lanes(fs[k])].astype(F32)
-        squares += jnp.sum(u * u, axis=1, keepdims=True)
-    r = lax.rsqrt(squares * (1.0 / depth) + 1e-06)
-    inner = jnp.zeros((hrows, 1), F32)
-    for k in range(4):
-        if k:
-            d_in[k].wait_recv()
-        u = tok[mine, lanes(fs[k])].astype(F32)
-        inner += jnp.sum(u * gains_all[k, 0:1, :] * drow[k].astype(F32), axis=1, keepdims=True)
-    pull = r * r * r * (inner * (1.0 / depth))
-    gpart[...] = gain_part[...]
-    for k in range(4):
-        at = lanes(fs[k])
-        u, d = tok[mine, at].astype(F32), drow[k].astype(F32)
-        gbuf[ti, :, at] = d_state[:, at] + (r * (gains_all[k, 0:1, :] * d) - u * pull)
-        gpart[k, 0:1, :] = jnp.sum(u * r * d, axis=0, keepdims=True)
-    g_side = wire(gbuf.at[ti], gbuf.at[ti], "tp", other)
-    g_in = {}
-    for k in (1, 2, 3):
-        g_in[k] = wire(gpart.at[k], gfar.at[k], "fsdp", fs[k])
-    line.push(2)
-    line.collect()
-    obuf[ti] = (state[...] + line.total[...]).astype(BF)
-    o_side = wire(obuf.at[ti], obuf.at[ti], "tp", other)
-    total = gpart[0]
-    for k in (1, 2, 3):
-        g_in[k].wait_recv()
-        total += gfar[k]
-    for step, (axis, peer) in enumerate((("ctx", cs[1]), ("ctx", cs[2]), ("tp", other))):
-        gsum[step] = total
-        copy = wire(gsum.at[step], gnear.at[step], axis, peer)
-        copy.wait_recv()
-        total = total + gnear[step]
-    gain_grads[...] = total
-    g_side.wait_recv()
-    grad_tok[...] = gbuf[...]
-    o_side.wait_recv()
-    out[...] = obuf[...]
-    line.drain()
-    wire.finish()
-
-
-def call_finish(part, state, tok, gains_all, gain_part, d_state, dq, dkv, w_q, w_kv, after):
-    hrows, depth = state.shape
-    rows, slab = 2 * hrows, depth // 4
-    shape = jax.ShapeDtypeStruct
-    vmem = pl.BlockSpec(memory_space=pltpu.VMEM)
-    hbm = pl.BlockSpec(memory_space=pl.ANY)
-    return pl.pallas_call(
-        finish_kernel,
-        out_shape=[
-            shape((2, hrows, depth), BF),
-            shape((2, hrows, depth), F32),
-            shape((8, slab), F32),
-        ],
-        in_specs=[vmem] * 10 + [hbm],
-        out_specs=[vmem] * 3,
-        scratch_shapes=[
-            pltpu.VMEM((4, hrows, depth), BF),
-            line_scratch(hrows, depth),
-            pltpu.VMEM((2, hrows, depth), BF),
-            pltpu.VMEM((2, hrows, depth), F32),
-            pltpu.VMEM((4, 2, hrows, slab), BF),
-            pltpu.VMEM((4, hrows, slab), BF),
-            pltpu.VMEM((4, hrows, slab), BF),
-            pltpu.VMEM((4, hrows, slab), BF),
-            pltpu.VMEM((4, 8, slab), F32),
-            pltpu.VMEM((4, 8, slab), F32),
-            pltpu.VMEM((3, 8, slab), F32),
-            pltpu.VMEM((3, 8, slab), F32),
-            pltpu.SemaphoreType.DMA((32,)),
-            pltpu.SemaphoreType.DMA((32,)),
-        ],
-        compiler_params=pltpu.CompilerParams(collective_id=6, has_side_effects=True),
-        cost_estimate=pl.CostEstimate(
-            flops=2 * 4 * rows * slab * w_q.shape[1], bytes_accessed=150_000_000, transcendentals=0
-        ),
-        name="finish",
-    )(part, state, tok, gains_all, gain_part, d_state, dq, dkv, w_q, w_kv, after)
 
 
 def fast_device(
@@ -1623,23 +1700,14 @@
         w_gate,
         w_up,
     )
-    down_full = call_gather(w_down, shard_down)
     normed_all = normed_all.reshape(length, depth)
     cot_all = cot_all.reshape(length, depth)
-    gate_full = gate_full.reshape(depth, units)
-    up_full = up_full.reshape(depth, units)
-    down_full = down_full.reshape(depth, units)
-
-    grad_down = lax.all_gather(shard_down, "ctx", axis=0, tiled=True)
-    d_hidden = matmul(cot_all, down_full)
-    _, geglu_pull = jax.vjp(geglu, gate, upward)
-    d_gate, d_up = geglu_pull(d_hidden)
-    d_gate = d_gate.astype(BF)
-    d_up = d_up.astype(BF)
-    dn = (times_transposed(d_gate, gate_full) + times_transposed(d_up, up_full)).astype(BF)
+    d_up, dn, part, shard_gate, down_all = call_middle(
+        w_down, shard_down, cot_all, normed_all, gate, upward, hidden, gate_full, up_full
+    )
     dn = dn.reshape(4, 2, hrows, depth)
-    part = times_transposed(hidden, down_full).astype(BF).reshape(4, 2, hrows, depth)
-    d_state, gain_part, dq, dkv, weight_grads, gate_all, up_all = call_backward(
+    part = part.reshape(4, 2, hrows, depth)
+    out, grad_tok, gain_grads, gate_all, up_all, weight_grads = call_backward(
         heads,
         dn,
         cot,
@@ -1654,14 +1722,15 @@
         normed_slab,
         att_plane,
         normed_all,
-        d_gate,
+        shard_gate,
         d_up,
-        shard_down,
-    )
-    weight_grads = lax.all_gather(weight_grads, "ctx", axis=0, tiled=False)
-    grad_gate, grad_up, grad_down = call_convert(gate_all, up_all, grad_down)
-    out, grad_tok, gain_grads = call_finish(
-        part, state, tok, gains_all, gain_part, d_state, dq, dkv, w_query, w_keyval, grad_gate
+        part,
+        tok,
+        w_query,
+        w_keyval,
+    )
+    grad_gate, grad_up, grad_down = call_convert(
+        gate_all, up_all, down_all.reshape(4 * units, slab)
     )
     quarter = heads * HD // 4
     grad_out = weight_grads[:, 0:quarter].reshape(4 * quarter, slab).astype(F32)

time: 809 us -> 632 us (0.78)
  waiting for transfers between devices: 141 us -> 0.01 us
  matrix products: 22.2 us -> 0 us
  between operations: 14.5 us -> 1.02 us
    all_gather x2 -> x0, waiting for transfers between devices: 140 us -> none  [the longest x1 79.2 us: fast_device(): grad_down = lax.all_gather(shard_down, 'ctx', axis=0, tiled=True)]
    dot_general x4 -> x0, matrix products: 22.2 us -> none  [the longest x3 14 us: times_transposed(): lax.dot_general(left, right, (((1,), (1,)), ((), ())), preferred_element_...]
    pallas_call x1, Pallas kernels: 283 us -> 293 us  [call_backward(): pl.pallas_call(functools.partial(backward_kernel, heads), out_shape=[shap...]
    pallas_call x2 -> x1, Pallas kernels: 101 us -> 95.5 us  [call_middle(): pl.pallas_call(middle_kernel, out_shape=[shape((length, units), BF), shap...]
  transfers between devices with their start and end apart: 3 -> 1, of which waited for: 2 -> 0; matrix products, arithmetic and copies ran while one was open for 3% -> 1% of each run, Pallas kernels for 0% -> 3%
where the time goes in v1:
time: 632 us; the launch traced here: 627 us
  Pallas kernels  604 us (96%)
  local copies, waits for them, and re-layouts  12.6 us (2%)
  other arithmetic  9.1 us (1%)
    pallas_call x1, Pallas kernels, call_backward(): pl.pallas_call(functools.partial(backward_kernel, heads), out_shape=[shap...  293 us
    pallas_call x1, Pallas kernels, call_forward(): pl.pallas_call(functools.partial(forward_kernel, heads), out_shape=[shape...  195 us
    pallas_call x1, Pallas kernels, call_middle(): pl.pallas_call(middle_kernel, out_shape=[shape((length, units), BF), shap...  95.5 us
    pallas_call x1, Pallas kernels, call_convert(): pl.pallas_call(convert_kernel, out_shape=[shape((slab, 4 * units), F32),...  20.8 us
  transfers between devices with their start and end apart: 1, of which 0 were waited for; matrix products, arithmetic and copies ran while one was open for 1% of the time, Pallas kernels for 3%

profile of v1, /device:TPU:0, one launch (start us, length us, event | category | flops | bytes accessed | tf_op | source)
XLA Modules:
  0.0 627.2 jit_solution(18235055151558507845)
XLA Ops:
  0.7 0.7 fusion.2
  1.4 0.9 convert_reduce_fusion
  2.3 0.3 fusion
  2.6 0.7 pad_maximum_fusion.cos
  3.3 0.7 broadcast_in_dim.6
  4.0 0.7 broadcast_in_dim.7
  4.7 0.8 and_convert_fusion.keep
  5.5 0.7 pad_maximum_fusion.1.sin
  6.3 0.1 pad.18.clone
  6.3 0.7 maximum_convert_fusion.gains
  7.0 194.9 %attention_forward.1 = (bf16[128,1280]{1,0:T(8,128)(2,1)}, bf16[2,4,128,256]{3,2,1,0:T(8,128)(2,1)}, f32[5,128,512]{2,1,0:T(8,128)}, f32[64,2560]{1,0:T(8,128)},...) custom-call(bf16[128,2560]{1,0:T(8,128)(2,1)} %bitcast.30, ...), custom_call_target="tpu_custom_call" | custom-call | flops 1845493760 | bytes 400000000 | tf_op jit(solution)/shard_map/attention_forward/pallas_call | solution.py:833
  202.0 95.5 %feed_forward_backward.1 = (bf16[512,960]{1,0:T(8,128)(2,1)}, bf16[512,2560]{1,0:T(8,128)(2,1)}, bf16[512,2560]{1,0:T(8,128)(2,1)}, bf16[640,960]{1,0:T(8,128)(2,1)}, bf16[4,960,640]{2,1,0:T(8,128)(2,1)}) custom-call(bf16[3840,640]{1,0:T(8,128)(2,1)} %w_down.1, bf16[960,640]{1,0:T(8,128)(2,1)} %get-tuple-element.39.shard_down, bf16[512,2560]{1,0:T(8,128)(2,1)} %bitcast.42, ...), custom_call_target="tpu_custom_call" | custom-call | flops 15099494400 | bytes 300000000 | tf_op jit(solution)/shard_map/feed_forward_backward/pallas_call | solution.py:516
  297.5 292.7 %attention_backward.1 = (bf16[2,64,2560]{2,1,0:T(8,128)(2,1)}, f32[2,64,2560]{2,1,0:T(8,128)}, f32[8,640]{1,0:T(8,128)}, bf16[4,640,960]{2,1,0:T(8,128)(2,1)}, b...) custom-call(bf16[4,2,64,2560]{3,2,1,0:T(8,128)(2,1)} %bitcast.36, bf16[128,2560]{1,0:T(8,128)(2,1)} %bitcast.33, ...), custom_call_target="tpu_custom_call" | custom-call | flops 838860800 | bytes 300000000 | tf_op jit(solution)/shard_map/attention_backward/pallas_call | solution.py:1478
  590.2 1.0 slice.16
  591.2 0.9 copy.23
  592.1 0.5 collective-permute-start
  592.6 2.2 fusion.5
  594.8 0.4 bitcast_convert_fusion.1
  595.2 2.1 bitcast_convert_fusion
  597.2 2.9 copy.21
  600.2 20.8 %convert.18 = (f32[640,3840]{1,0:T(8,128)}, f32[640,3840]{1,0:T(8,128)}, f32[3840,640]{1,0:T(8,128)}) custom-call(bf16[4,640,960]{2,1,0:T(8,128)(2,1)} %get-tuple-element.61.gate_all, bf16[4,640,960]{2,1,0:T(8,128)(2,1)} %get-tuple-element.62.up_all, bf16[3840,640]{1,0:T(8,128)(2,1)} %bitcast.28), custom_call_target="tpu_custom_call" | custom-call | bytes 44236800 | tf_op jit(solution)/shard_map/convert/pallas_call | solution.py:1605
  621.0 0.0 copy-start.1
  621.0 0.0 copy-start
  621.0 1.5 slice_reduce_fusion
  622.5 0.0 collective-permute-done
  622.5 2.5 convert_bitcast_fusion
  625.1 0.0 copy-done.1
  625.1 0.8 copy.27
  625.9 0.0 copy-done
  625.9 1.1 copy.28
  (7 shorter events, 0.1 us)
Async XLA Ops:
  592.1 30.4 %collective-permute-start = (bf16[256,640]{0,1:T(8,128)(2,1)}, bf16[256,640]{0,1:T(8,128)(2,1)}, u32[]{:S(2)}, u32[]{:S(2)}) collective-permute-start(bf16[256,640]{0,1:T(8,128)(2,1)} %copy.23), channel_id=1, source_target_pairs={{0,1},{1,0},{2,3},{3,2},{4,5},{5,4},{6,7},{7,6},{8,9},{9,8},{10,11... | collective-permute-start | bytes 983048 | tf_op jit(solution)/shard_map/ppermute | solution.py:52
  621.0 4.1 copy-start.1
  621.0 4.9 copy-start

commit v2 on v1

--- a/solution.py
+++ b/solution.py
@@ -407,7 +407,6 @@
     part,
     shard_gate,
     down_all,
-    down_rows,
     dfull,
     cot,
     normed,
@@ -429,13 +428,13 @@
 ):
     fs, cs = partners("fsdp", 4), partners("ctx", 4)
     ci = lax.axis_index("ctx")
-    units, slab = down_rows.shape
+    units, slab = dfull.shape[1:]
     length, _ = cot.shape
     loads = [
         pltpu.make_async_copy(source, target, local.at[n])
         for n, (source, target) in enumerate(
             (
-                (w_down.at[pl.ds(pl.multiple_of(ci * units, 64), units), :], down_rows),
+                (w_down.at[pl.ds(pl.multiple_of(ci * units, 64), units), :], dfull.at[fs[0]]),
                 (cot_in, cot),
                 (gate_in, gate),
                 (up_in, upward),
@@ -455,11 +454,10 @@
     spread.begin()
     for p in range(PIECES):
         spread.give(p)
-    gather = Gather(wire, fs, 8, slab // 8, lambda m, index, at: dfull.at[index, at, :])
+    gather = Gather(wire, fs, 10, units // 10, lambda m, index, at: dfull.at[index, at, :])
 
     def prepare(m):
         loads[0].wait()
-        dfull[fs[0]] = down_rows[...].T
 
     def lanes(index):
         return pl.ds(pl.multiple_of(index * slab, slab), slab)
@@ -467,14 +465,14 @@
     for n, _ in enumerate(gather.steps((0,), prepare)):
         if n == 3:
             loads[1].wait()
-            dh[...] = jnp.dot(cot[:, lanes(fs[0])], dfull[fs[0]], preferred_element_type=F32)
-        if n >= 8:
-            spread.hand_on(n - 8)
+            dh[...] = nt_dot(cot[:, lanes(fs[0])], dfull[fs[0]])
+        if n >= 15 - PIECES:
+            spread.hand_on(n - 15 + PIECES)
     for load in loads[2:]:
         load.wait()
     gather.settle()
     for k in (1, 2, 3):
-        dh[...] += jnp.dot(cot[:, lanes(fs[k])], dfull[fs[k]], preferred_element_type=F32)
+        dh[...] += nt_dot(cot[:, lanes(fs[k])], dfull[fs[k]])
     step = 128
     for n in range(length // step):
         at = slice(n * step, (n + 1) * step)
@@ -487,18 +485,21 @@
         )
         d_gate[at, :] = (d * upward[at, :] * slope).astype(BF)
         d_up[at, :] = (d * (v * cdf)).astype(BF)
-    product = Product(wire, False, normed, d_gate, shard_gate, parts, near, far, sums)
+    product = Product(wire, True, d_gate, normed, shard_gate, parts, near, far, sums)
     product.start()
     for p in range(PIECES // 2):
         spread.hand_far(p)
     for j in range(4):
-        block = nt_dot(d_gate[...], gate_w[j]) + nt_dot(d_up[...], up_w[j])
+        block = jnp.dot(d_gate[...], gate_w[j], preferred_element_type=F32)
+        block += jnp.dot(d_up[...], up_w[j], preferred_element_type=F32)
         dn[:, j * slab : (j + 1) * slab] = block.astype(BF)
     product.middle()
     for p in range(PIECES // 2, PIECES):
         spread.hand_far(p)
     for j in range(4):
-        part[:, j * slab : (j + 1) * slab] = nt_dot(hidden[...], dfull[j]).astype(BF)
+        part[:, j * slab : (j + 1) * slab] = jnp.dot(
+            hidden[...], dfull[j], preferred_element_type=F32
+        ).astype(BF)
     product.end()
     spread.close()
     wire.finish()
@@ -507,7 +508,7 @@
 def call_middle(w_down, shard_down, cot, normed, gate, upward, hidden, gate_w, up_w):
     units, slab = shard_down.shape
     length, depth = cot.shape
-    sizes = product_sizes(False, slab, units)
+    sizes = product_sizes(True, slab, units)
     pair = [pltpu.VMEM((2, *size), BF) for size in sizes]
     single = [pltpu.VMEM(size, BF) for size in sizes]
     shape = jax.ShapeDtypeStruct
@@ -519,21 +520,20 @@
             shape((length, units), BF),
             shape((length, depth), BF),
             shape((length, depth), BF),
-            shape((slab, units), BF),
+            shape((units, slab), BF),
             shape((4, units, slab), BF),
         ],
         in_specs=[hbm] * 9,
         out_specs=[vmem] * 4 + [hbm],
         scratch_shapes=[
-            pltpu.VMEM((units, slab), BF),
-            pltpu.VMEM((4, slab, units), BF),
+            pltpu.VMEM((4, units, slab), BF),
             pltpu.VMEM((length, depth), BF),
             pltpu.VMEM((length, depth), BF),
             pltpu.VMEM((length, units), F32),
             pltpu.VMEM((length, units), F32),
             pltpu.VMEM((length, units), BF),
-            pltpu.VMEM((4, slab, units), BF),
-            pltpu.VMEM((4, slab, units), BF),
+            pltpu.VMEM((4, units, slab), BF),
+            pltpu.VMEM((4, units, slab), BF),
             pltpu.VMEM((length, units), F32),
             pltpu.VMEM((length, units), BF),
             list(pair),
@@ -541,8 +541,8 @@
             list(single),
             list(single),
             spread_scratch(PIECES),
-            pltpu.SemaphoreType.DMA((32,)),
-            pltpu.SemaphoreType.DMA((32,)),
+            pltpu.SemaphoreType.DMA((40,)),
+            pltpu.SemaphoreType.DMA((40,)),
             pltpu.SemaphoreType.DMA((8,)),
         ],
         compiler_params=pltpu.CompilerParams(
@@ -614,7 +614,7 @@
     slab = depth // 4
     hrows = rows // 2
     qcols = heads * HD
-    units = gate_full.shape[2]
+    units = gate_full.shape[1]
     scale = HD ** (-0.5)
     wire = Wire(send, recv)
     locals_ = []
@@ -642,7 +642,7 @@
 
     x_in = [None] * 4
     for k in (1, 2, 3):
-        x_in[k] = wire(tok.at[:, lanes(fs[k])], xbuf.at[k], "fsdp", fs[k])
+        x_in[k] = wire(tok.at[mine, lanes(fs[k])], xbuf.at[k, mine, :], "fsdp", fs[k])
     g_in = [None] * 4
     for k in (1, 2, 3):
         g_in[k] = wire(gains, grel.at[k], "fsdp", fs[k])
@@ -653,7 +653,7 @@
     rbuf[0] = jnp.broadcast_to(r, (rows, 128))
     r_in = [None] * 4
     for k in (1, 2, 3):
-        r_in[k] = wire(rbuf.at[0], rbuf.at[k], "fsdp", fs[k])
+        r_in[k] = wire(rbuf.at[0, mine, :], rbuf.at[k, mine, :], "fsdp", fs[k])
     c_in = [None] * 4
     for k in (1, 2, 3):
         c_in[k] = wire(cot.at[mine, :], call.at[ci, ti], "ctx", cs[k])
@@ -661,8 +661,8 @@
         call[ci, half] = cot[half * hrows : (half + 1) * hrows, :]
 
     odd = units % 128
-    pieces = 8
-    height = slab // pieces
+    pieces = 10
+    height = units // pieces
 
     def prepare(m):
         win[m].wait()
@@ -670,13 +670,13 @@
 
             @pl.when(lax.rem(ci, 2) == 0)
             def _():
-                wfull[m, fs[0]] = window[m, :, 0:units]
+                wfull[m, fs[0]] = window[m, :, 0:units].T
 
             @pl.when(lax.rem(ci, 2) == 1)
             def _():
-                wfull[m, fs[0]] = window[m, :, odd : odd + units]
+                wfull[m, fs[0]] = window[m, :, odd : odd + units].T
         else:
-            wfull[m, fs[0]] = window[m, :, 0:units]
+            wfull[m, fs[0]] = window[m, :, 0:units].T
 
     gather = Gather(wire, fs, pieces, height, lambda m, index, at: wfull.at[m, index, at, :])
     schedule = gather.steps((0, 1), prepare)
@@ -689,10 +689,18 @@
     gain_one = gains[0:1, :]
     kv_half = w_kv[:, pl.ds(pl.multiple_of(ti * HD, HD), HD)]
     p_in = [None] * 4
+    pass_x = {}
     for k in range(4):
+        if k == 1:
+            for j in (1, 2, 3):
+                x_in[j].wait_recv()
+                r_in[j].wait_recv()
+                for buffer in (xbuf, rbuf):
+                    half = buffer.at[j, mine, :]
+                    pass_x[j, buffer is rbuf] = wire(half, half, "tp", other)
         if k:
-            x_in[k].wait_recv()
-            r_in[k].wait_recv()
+            pass_x[k, False].wait_recv()
+            pass_x[k, True].wait_recv()
         normed = (xbuf[k].astype(F32) * wide(rbuf[k], slab) * gain_one).astype(BF)
         normed_slab[k] = normed
         part[k, :, 0:qcols] = jnp.dot(normed, w_q[...], preferred_element_type=F32).astype(BF)
@@ -738,8 +746,8 @@
         attbuf[0, :, h * HD : (h + 1) * HD] = jnp.dot(
             p.astype(BF), values, preferred_element_type=F32
         ).astype(BF)
-    a_in = [None] * 4
-    for k in (1, 2, 3):
+    a_in = {}
+    for k in (1, 2):
         a_in[k] = wire(attbuf.at[0], attbuf.at[k], "fsdp", fs[k])
     bulk(BULK[3])
     c_side = []
@@ -748,8 +756,18 @@
         c_side.append(wire(call.at[cs[k], ti], call.at[cs[k], ti], "tp", other))
     o_in = []
     for k in range(4):
-        if k:
-            a_in[k].wait_recv()
+        if k == 1:
+            for j, to, start in ((1, 2, 0), (2, 1, hrows)):
+                a_in[j].wait_recv()
+                a_in[3, j] = wire(
+                    attbuf.at[j, pl.ds(start, hrows), :],
+                    attbuf.at[3, pl.ds(start, hrows), :],
+                    "fsdp",
+                    fs[to],
+                )
+        if k == 3:
+            a_in[3, 1].wait_recv()
+            a_in[3, 2].wait_recv()
         att_plane[k] = attbuf[k]
         block = jnp.dot(attbuf[k], w_o[...], preferred_element_type=F32).astype(BF)
         obuf[k, 0] = block[0:hrows]
@@ -789,19 +807,26 @@
         n_side.append(wire(nall.at[cs[k], ti], nall.at[cs[k], ti], "tp", other))
         bulk(BULK[6])
     bulk(1000)
+    for copy in n_side:
+        copy.wait_recv()
+
+    def project(f):
+        x = nall[:, :, :, lanes(f)].reshape(length, slab)
+        return nt_dot(x, wfull[0, f]), nt_dot(x, wfull[1, f])
+
+    gate[...], upward[...] = project(fs[0])
     gather.settle()
     keep_local(wfull.at[0], gate_full)
     keep_local(wfull.at[1], up_full)
+    for k in (1, 2, 3):
+        g, u = project(fs[k])
+        gate[...] += g
+        upward[...] += u
     for k in range(4):
-        n_side[k].wait_recv()
-        x = nall[cs[k]].reshape(rows, depth)
-        at = pl.ds(pl.multiple_of(cs[k] * rows, rows), rows)
-        g = jnp.dot(x, wfull[0].reshape(depth, units), preferred_element_type=F32)
-        u = jnp.dot(x, wfull[1].reshape(depth, units), preferred_element_type=F32)
-        gate[at, :] = g
-        upward[at, :] = u
+        at = slice(k * rows, (k + 1) * rows)
+        g = gate[at, :]
         cdf = 0.5 * (1.0 + jnp.tanh(0.7978845608028654 * (g + 0.044715 * (g * g * g))))
-        hidden[at, :] = (g * cdf * u).astype(BF)
+        hidden[at, :] = (g * cdf * upward[at, :]).astype(BF)
     keep_local(nall, normed_all)
     for copy in c_side:
         copy.wait_recv()
@@ -815,7 +840,7 @@
     wire.finish()
 
 
-BULK = (3, 4, 3, 3, 3, 6, 1)
+BULK = (4, 5, 4, 4, 4, 7, 1)
 
 
 def call_forward(heads, tok, cot, gains, cos, sin, keep, w_q, w_kv, w_o, w_gate, w_up):
@@ -840,8 +865,8 @@
             shape((4, 8, slab), F32),
             shape((4, 2, hrows, depth), BF),
             shape((4, 2, hrows, depth), BF),
-            shape((4, slab, units), BF),
-            shape((4, slab, units), BF),
+            shape((4, units, slab), BF),
+            shape((4, units, slab), BF),
             shape((4, rows, slab), BF),
             shape((4, rows, qcols), BF),
             shape((length, units), F32),
@@ -865,7 +890,7 @@
             pltpu.VMEM((hrows, depth), BF),
             pltpu.VMEM((4, 8, slab), F32),
             pltpu.VMEM((2, slab, reach), BF),
-            pltpu.VMEM((2, 4, slab, units), BF),
+            pltpu.VMEM((2, 4, units, slab), BF),
             pltpu.VMEM((4, 2, hrows, depth), BF),
             pltpu.VMEM((4, 2, hrows, depth), BF),
             list(pair),
@@ -992,16 +1017,16 @@
         self.outbox[way, slot] = (self.own(u) + self.inbox[way, slot].astype(F32)).astype(BF)
         self.copy(way, u).start()
 
-    def push_near(self):
-        @pl.when(self.ci == 1)
-        def _():
-            self.hop(0, 3)
-            self.hop(0, 2)
-
-        @pl.when(self.ci == 2)
-        def _():
-            self.hop(1, 0)
-            self.hop(1, 1)
+    def push_near(self, steps=(0, 1)):
+        for step in steps:
+
+            @pl.when(self.ci == 1)
+            def _():
+                self.hop(0, 3 - step)
+
+            @pl.when(self.ci == 2)
+            def _():
+                self.hop(1, step)
 
     def push_far(self):
         @pl.when(self.ci == 1)
@@ -1148,30 +1173,31 @@
 def backward_kernel(
     heads,
     dn,
-    cot,
+    cot_in,
     state,
     gains_all,
-    probs,
-    q_rot,
-    kv,
+    probs_in,
+    q_rot_in,
+    kv_in,
     cos,
     sin,
-    w_o,
-    normed,
-    att,
+    w_o_in,
+    normed_in,
+    att_in,
     normed_all,
     shard_gate,
     d_up,
-    part,
-    tok,
-    w_q,
-    w_kv,
+    part_in,
+    tok_in,
+    w_q_in,
+    w_kv_in,
     out,
     grad_tok,
     gain_grads,
     gate_all,
     up_all,
     weights_all,
+    kv_side,
     side,
     dbuf,
     dslab,
@@ -1210,6 +1236,8 @@
     gsum,
     gnear,
     gall,
+    late,
+    late_sems,
     send,
     recv,
     local,
@@ -1222,6 +1250,12 @@
     slab = depth // 4
     length = 4 * rows
     scale = HD ** (-0.5)
+    sources = (cot_in, probs_in, q_rot_in, kv_in, w_o_in, normed_in, att_in, part_in, tok_in, w_q_in, w_kv_in)
+    cot, probs, q_rot, kv, w_o, normed, att, part, tok, w_q, w_kv = late
+    loads = [
+        pltpu.make_async_copy(source, target, late_sems.at[n])
+        for n, (source, target) in enumerate(zip(sources, late))
+    ]
     greet(
         [("fsdp", fs[k]) for k in (1, 2, 3)]
         + [("ctx", cs[k]) for k in (1, 2, 3)]
@@ -1233,7 +1267,7 @@
     def lanes(index):
         return pl.ds(pl.multiple_of(index * slab, slab), slab)
 
-    up = Product(wire, False, normed_all, d_up, shard_up, parts, *product_recv, sums)
+    up = Product(wire, True, d_up, normed_all, shard_up, parts, *product_recv, sums)
     gate_line = Spread(shard_gate, gate_all, PIECES, *gate_sems)
     up_line = Spread(shard_up, up_all, PIECES, *up_sems)
     line = units_line(wire, dn, side, row_refs, ti)
@@ -1241,6 +1275,8 @@
     gate_line.begin()
     for p in range(PIECES // 2):
         gate_line.give(p)
+    for load in loads:
+        load.start()
     up.start()
     squares = jnp.zeros((hrows, 1), F32)
     for k in range(4):
@@ -1251,8 +1287,9 @@
     line.push_far()
     for p in range(PIECES // 2, PIECES):
         gate_line.give(p)
-    up.middle()
     line.collect()
+    for load in loads:
+        load.wait()
     inner = jnp.zeros((hrows, 1), F32)
     for k in range(4):
         at = lanes(fs[k])
@@ -1275,6 +1312,7 @@
             dslab[0, ti] = ds.astype(BF)
             d_side[0] = wire(dslab.at[0, ti], dslab.at[0, ti], "tp", other)
         gpart[k, 1:2, :] = jnp.sum(u * r * d, axis=0, keepdims=True)
+    up.middle()
     for k in (1, 2, 3):
         d_in[k].wait_recv()
         d_side[k] = wire(dslab.at[k, ti], dslab.at[k, ti], "tp", other)
@@ -1346,10 +1384,10 @@
     v_in = {}
     for k in (1, 2, 3):
         v_in[k] = wire(dkvbuf.at[0], dkvbuf.at[k], "fsdp", fs[k])
+    out_line.push_near()
     up_line.begin()
     for p in range(PIECES):
         up_line.give(p)
-    out_line.push_near()
     for k in (1, 2, 3):
         q_in[k].wait_recv()
     slabs = normed[...].reshape(length, slab)
@@ -1387,11 +1425,7 @@
     r = lax.rsqrt(squares * (1.0 / depth) + 1e-06)
     for p in range(PIECES):
         up_line.hand_on(p)
-    line.drain()
-    last = units_line(wire, part, side, [*row_refs[:3], *last_sems], ti)
-    last.lead()
-    for p in range(PIECES // 2):
-        up_line.hand_far(p)
+    query_line.push_near((0,))
     inner = jnp.zeros((hrows, 1), F32)
     for k in range(4):
         if k:
@@ -1408,9 +1442,12 @@
     g_in = {}
     for k in (1, 2, 3):
         g_in[k] = wire(gpart.at[k], gfar.at[k], "fsdp", fs[k])
+    for p in range(PIECES // 2):
+        up_line.hand_far(p)
+    query_line.push_far()
+    query_line.push_near((1,))
     for p in range(PIECES // 2, PIECES):
         up_line.hand_far(p)
-    query_line.push_near()
     gain_sum = gpart[0]
     for k in (1, 2, 3):
         g_in[k].wait_recv()
@@ -1420,8 +1457,6 @@
     near_gain.wait_recv()
     gall[ci] = gain_sum + gnear[...]
     all_gain = [wire(gall.at[ci], gall.at[ci], "ctx", cs[k]) for k in (1, 2, 3)]
-    query_line.push_far()
-    last.push_near()
     out_line.collect()
     weight_grads[0:quarter, :] = out_line.total[...].astype(BF)
     query_line.collect()
@@ -1430,16 +1465,20 @@
     weight_line.begin()
     for p in range(PIECES):
         weight_line.give(p)
-    last.push_far()
+    line.drain()
+    last = units_line(wire, part, side, [*row_refs[:3], *last_sems], ti)
+    last.lead()
     for p in range(PIECES):
         weight_line.hand_on(p)
+    last.push_near()
     for p in range(PIECES // 2):
+        weight_line.hand_far(p)
+    last.push_far()
+    for p in range(PIECES // 2, PIECES):
         weight_line.hand_far(p)
     last.collect()
     obuf[ti] = (state[...] + last.total[...]).astype(BF)
     o_side = wire(obuf.at[ti], obuf.at[ti], "tp", other)
-    for p in range(PIECES // 2, PIECES):
-        weight_line.hand_far(p)
     t_side.wait_recv()
     keep_t = pltpu.make_async_copy(gbuf, grad_tok, local.at[0])
     keep_t.start()
@@ -1452,6 +1491,9 @@
     gate_line.close()
     up_line.close()
     weight_line.close()
+    tail = pl.ds(2 * quarter, HD // 4)
+    kv_last = wire(weights_all.at[:, tail, :], kv_side, "tp", other)
+    kv_last.wait_recv()
     for each in (last, out_line, query_line):
         each.drain()
     keep_t.wait()
@@ -1469,7 +1511,8 @@
     rows, slab, qcols = 2 * hrows, depth // 4, heads * HD
     length = 4 * rows
     units = d_up.shape[1]
-    sizes = product_sizes(False, slab, units)
+    late = (cot, probs, q_rot, kv, w_o, normed, att, part, tok, w_q, w_kv)
+    sizes = product_sizes(True, slab, units)
     pair = [pltpu.VMEM((2, *size), BF) for size in sizes]
     single = [pltpu.VMEM(size, BF) for size in sizes]
     shape = jax.ShapeDtypeStruct
@@ -1481,12 +1524,16 @@
             shape((2, hrows, depth), BF),
             shape((2, hrows, depth), F32),
             shape((8, slab), F32),
-            shape((4, slab, units), BF),
-            shape((4, slab, units), BF),
+            shape((4, units, slab), BF),
+            shape((4, units, slab), BF),
             shape((4, qcols // 2 + HD // 4, slab), BF),
+            shape((4, HD // 4, slab), BF),
         ],
-        in_specs=[vmem] * 13 + [hbm] + [vmem] * 5,
-        out_specs=[hbm] * 2 + [vmem] + [hbm] * 3,
+        in_specs=[vmem, hbm, vmem, vmem, hbm, hbm, hbm, vmem, vmem]
+        + [hbm] * 3
+        + [vmem, hbm, vmem]
+        + [hbm] * 4,
+        out_specs=[hbm] * 2 + [vmem] + [hbm] * 4,
         scratch_shapes=[
             pltpu.VMEM((4, hrows, depth), BF),
             pltpu.VMEM((4, hrows, slab), BF),
@@ -1509,7 +1556,7 @@
             list(pair),
             list(single),
             [list(pair), list(single)],
-            pltpu.VMEM((slab, units), BF),
+            pltpu.VMEM((units, slab), BF),
             spread_scratch(PIECES),
             spread_scratch(PIECES),
             pltpu.VMEM((4, 8, slab), F32),
@@ -1526,6 +1573,8 @@
             pltpu.VMEM((8, slab), F32),
             pltpu.VMEM((8, slab), F32),
             pltpu.VMEM((4, 8, slab), F32),
+            [pltpu.VMEM(each.shape, each.dtype) for each in late],
+            pltpu.SemaphoreType.DMA((len(late),)),
             pltpu.SemaphoreType.DMA((64,)),
             pltpu.SemaphoreType.DMA((64,)),
             pltpu.SemaphoreType.DMA((2,)),
@@ -1540,66 +1589,151 @@
     )(dn, cot, state, gains_all, probs, q_rot, kv, cos, sin, w_o, normed, att, normed_all, shard_gate, d_up, part, tok, w_q, w_kv)
 
 
-STRIP = 80
-
-
-def conversions(sources, targets, inbuf, outbuf, in_sems, out_sems):
-    jobs = []
-    for which in (0, 1):
-        for p in range(sources[which].shape[1] // STRIP):
-            jobs.append((which, p))
-    for p in range(sources[2].shape[0] // (4 * STRIP)):
-        jobs.append((2, p))
-
-    def load(n):
-        which, p = jobs[n]
-        slot = n % 2
-        if which < 2:
-            source = sources[which].at[:, pl.ds(p * STRIP, STRIP), :]
-            return pltpu.make_async_copy(source, inbuf[0].at[slot], in_sems.at[slot])
-        source = sources[2].at[pl.ds(p * 4 * STRIP, 4 * STRIP), :]
-        return pltpu.make_async_copy(source, inbuf[1].at[slot], in_sems.at[slot])
-
-    def store(n):
-        which, p = jobs[n]
-        slot = n % 2
-        if which < 2:
-            target = targets[which].at[pl.ds(p * STRIP, STRIP), :]
-            return pltpu.make_async_copy(outbuf[0].at[slot], target, out_sems.at[slot])
-        target = targets[2].at[pl.ds(p * 4 * STRIP, 4 * STRIP), :]
-        return pltpu.make_async_copy(outbuf[1].at[slot], target, out_sems.at[slot])
-
-    load(0).start()
-    for n, (which, p) in enumerate(jobs):
-        slot = n % 2
-        if n + 1 < len(jobs):
-            load(n + 1).start()
-        load(n).wait()
-        if n >= 2:
-            store(n - 2).wait()
-        if which < 2:
-            units = sources[which].shape[2]
-            for j in range(4):
-                outbuf[0][slot, :, j * units : (j + 1) * units] = inbuf[0][slot, j].astype(F32)
-        else:
-            outbuf[1][slot] = inbuf[1][slot].astype(F32)
-        store(n).start()
-        if n + 1 == len(jobs):
-            store(n - 1).wait()
-            store(n).wait()
-        yield
-
-
-def convert_kernel(gate_all, up_all, down_all, grad_gate, grad_up, grad_down, inbuf, outbuf, in_sems, out_sems):
-    steps = conversions(
-        (gate_all, up_all, down_all), (grad_gate, grad_up, grad_down), inbuf, outbuf, in_sems, out_sems
-    )
-    for _ in steps:
-        pass
-
-
-def call_convert(gate_all, up_all, down_all):
-    slab, units = gate_all.shape[1:]
+STRIP = 128
+
+
+def convert_kernel(
+    gate_all,
+    up_all,
+    down_all,
+    weights_all,
+    kv_side,
+    out_in,
+    tok_in,
+    grad_gate,
+    grad_up,
+    grad_down,
+    grad_out,
+    grad_query,
+    grad_kv,
+    out,
+    grad_tok,
+    wide_in,
+    wide_out,
+    tall_in,
+    tall_out,
+    turn_in,
+    turn_out,
+    kv_in,
+    kv_out,
+    same_out,
+    same_tok,
+    in_sems,
+    out_sems,
+):
+    ti = lax.axis_index("tp")
+    units, slab = gate_all.shape[1:]
+    quarter = grad_query.shape[1] // 4
+    loads, works, stores = [], [], []
+
+    def job(sources, work, target_from, target):
+        n = len(loads)
+        slot = n % 3
+        loads.append(
+            [
+                pltpu.make_async_copy(source, place(slot), in_sems.at[slot, m])
+                for m, (source, place) in enumerate(sources)
+            ]
+        )
+        works.append(lambda: work(slot))
+        stores.append(pltpu.make_async_copy(target_from(slot), target, out_sems.at[slot]))
+
+    def strips(source, target):
+        for p in range(slab // STRIP):
+            rows = pl.ds(p * STRIP, STRIP)
+
+            def work(slot):
+                block = wide_in[slot].reshape(4 * units, STRIP)
+                for j in range(6):
+                    at = slice(j * 4 * units // 6, (j + 1) * 4 * units // 6)
+                    wide_out[slot, :, at] = block[at].T.astype(F32)
+
+            job(
+                [(source.at[:, :, rows], lambda slot: wide_in.at[slot])],
+                work,
+                lambda slot: wide_out.at[slot],
+                target.at[rows, :],
+            )
+
+    def tall_work(slot):
+        tall_out[slot] = tall_in[slot].astype(F32)
+
+    def low_work(slot):
+        tall_out[slot, 0:quarter] = tall_in[slot, 0:quarter].astype(F32)
+
+    strips(gate_all, grad_gate)
+    strips(up_all, grad_up)
+    high = tall_in.shape[1]
+    for p in range(4 * units // high):
+        rows = pl.ds(p * high, high)
+        job(
+            [(down_all.at[rows, :], lambda slot: tall_in.at[slot])],
+            tall_work,
+            lambda slot: tall_out.at[slot],
+            grad_down.at[rows, :],
+        )
+    for j in range(4):
+        part = pl.ds(0, quarter)
+        job(
+            [(weights_all.at[j, part, :], lambda slot: tall_in.at[slot, part, :])],
+            low_work,
+            lambda slot: tall_out.at[slot, part, :],
+            grad_out.at[pl.ds(j * quarter, quarter), :],
+        )
+    early = [
+        pltpu.make_async_copy(
+            weights_all.at[j, pl.ds(quarter, quarter), :],
+            turn_in.at[pl.ds(j * quarter, quarter), :],
+            in_sems.at[3, j],
+        )
+        for j in range(4)
+    ] + [
+        pltpu.make_async_copy(
+            weights_all.at[:, pl.ds(2 * quarter, HD // 4), :], kv_in.at[0], in_sems.at[4, 0]
+        ),
+        pltpu.make_async_copy(kv_side, kv_in.at[1], in_sems.at[4, 1]),
+    ]
+    same = [
+        pltpu.make_async_copy(out_in, same_out, in_sems.at[4, 2]),
+        pltpu.make_async_copy(tok_in, same_tok, in_sems.at[4, 3]),
+    ]
+    for copy in loads[0] + loads[1] + early + same:
+        copy.start()
+    for n in range(len(loads)):
+        if n + 2 < len(loads):
+            for copy in loads[n + 2]:
+                copy.start()
+        for copy in loads[n]:
+            copy.wait()
+        if n >= 3:
+            stores[n - 3].wait()
+        works[n]()
+        stores[n].start()
+    late = []
+    for n, (copy, source, target) in enumerate(
+        ((same[0], same_out, out), (same[1], same_tok, grad_tok))
+    ):
+        copy.wait()
+        late.append(pltpu.make_async_copy(source, target, out_sems.at[3 + n]))
+        late[-1].start()
+    for copy in early:
+        copy.wait()
+    for i in range(4 * quarter // 256):
+        turn_out[:, i * 256 : (i + 1) * 256] = turn_in[i * 256 : (i + 1) * 256, :].T.astype(F32)
+    late.append(pltpu.make_async_copy(turn_out, grad_query, out_sems.at[5]))
+    late[-1].start()
+    for n, place in ((0, ti), (1, 1 - ti)):
+        at = pl.ds(pl.multiple_of(place * HD, HD), HD)
+        kv_out[:, at] = kv_in[n].reshape(HD, slab).T.astype(F32)
+    late.append(pltpu.make_async_copy(kv_out, grad_kv, out_sems.at[6]))
+    late[-1].start()
+    for copy in stores[-3:] + late:
+        copy.wait()
+
+
+def call_convert(gate_all, up_all, down_all, weights_all, kv_side, out, grad_tok):
+    units, slab = gate_all.shape[1:]
+    quarter = (weights_all.shape[1] - HD // 4) // 2
     shape = jax.ShapeDtypeStruct
     hbm = pl.BlockSpec(memory_space=pl.ANY)
     return pl.pallas_call(
@@ -1608,20 +1742,34 @@
             shape((slab, 4 * units), F32),
             shape((slab, 4 * units), F32),
             shape((4 * units, slab), F32),
+            shape((4 * quarter, slab), F32),
+            shape((slab, 4 * quarter), F32),
+            shape((slab, 2 * HD), F32),
+            shape(out.shape, out.dtype),
+            shape(grad_tok.shape, grad_tok.dtype),
         ],
-        in_specs=[hbm] * 3,
-        out_specs=[hbm] * 3,
+        in_specs=[hbm] * 7,
+        out_specs=[hbm] * 8,
         scratch_shapes=[
-            [pltpu.VMEM((2, 4, STRIP, units), BF), pltpu.VMEM((2, 4 * STRIP, slab), BF)],
-            [pltpu.VMEM((2, STRIP, 4 * units), F32), pltpu.VMEM((2, 4 * STRIP, slab), F32)],
-            pltpu.SemaphoreType.DMA((2,)),
-            pltpu.SemaphoreType.DMA((2,)),
+            pltpu.VMEM((3, 4, units, STRIP), BF),
+            pltpu.VMEM((3, STRIP, 4 * units), F32),
+            pltpu.VMEM((3, units, slab), BF),
+            pltpu.VMEM((3, units, slab), F32),
+            pltpu.VMEM((4 * quarter, slab), BF),
+            pltpu.VMEM((slab, 4 * quarter), F32),
+            pltpu.VMEM((2, 4, HD // 4, slab), BF),
+            pltpu.VMEM((slab, 2 * HD), F32),
+            pltpu.VMEM(out.shape, out.dtype),
+            pltpu.VMEM(grad_tok.shape, grad_tok.dtype),
+            pltpu.SemaphoreType.DMA((5, 4)),
+            pltpu.SemaphoreType.DMA((7,)),
         ],
+        compiler_params=pltpu.CompilerParams(vmem_limit_bytes=67_043_328),
         cost_estimate=pl.CostEstimate(
-            flops=0, bytes_accessed=18 * slab * 4 * units, transcendentals=0
+            flops=0, bytes_accessed=20 * slab * 4 * units, transcendentals=0
         ),
         name="convert",
-    )(gate_all, up_all, down_all)
+    )(gate_all, up_all, down_all, weights_all, kv_side, out, grad_tok)
 
 
 def fast_device(
@@ -1637,7 +1785,7 @@
     gain_ffn,
     cotangent,
 ):
-    ci, ti = lax.axis_index("ctx"), lax.axis_index("tp")
+    ci = lax.axis_index("ctx")
     tok, cot = tokens[0], cotangent[0]
     rows, depth = tok.shape
     hrows, slab = rows // 2, depth // 4
@@ -1707,7 +1855,7 @@
     )
     dn = dn.reshape(4, 2, hrows, depth)
     part = part.reshape(4, 2, hrows, depth)
-    out, grad_tok, gain_grads, gate_all, up_all, weight_grads = call_backward(
+    out, grad_tok, gain_grads, gate_all, up_all, weight_grads, kv_side = call_backward(
         heads,
         dn,
         cot,
@@ -1729,19 +1877,24 @@
         w_query,
         w_keyval,
     )
-    grad_gate, grad_up, grad_down = call_convert(
-        gate_all, up_all, down_all.reshape(4 * units, slab)
-    )
-    quarter = heads * HD // 4
-    grad_out = weight_grads[:, 0:quarter].reshape(4 * quarter, slab).astype(F32)
-    grad_query = weight_grads[:, quarter : 2 * quarter].reshape(4 * quarter, slab).T.astype(F32)
-    kv_mine = weight_grads[:, 2 * quarter :].reshape(HD, slab)
-    kv_other = swap(kv_mine, "tp", 2, 1)
-    grad_kv = jnp.where(
-        ti == 0,
-        jnp.concatenate([kv_mine, kv_other], axis=0),
-        jnp.concatenate([kv_other, kv_mine], axis=0),
-    ).T.astype(F32)
+    (
+        grad_gate,
+        grad_up,
+        grad_down,
+        grad_out,
+        grad_query,
+        grad_kv,
+        out,
+        grad_tok,
+    ) = call_convert(
+        gate_all,
+        up_all,
+        down_all.reshape(4 * units, slab),
+        weight_grads,
+        kv_side,
+        out,
+        grad_tok,
+    )
 
     return (
         out.reshape(1, rows, depth),

time: 632 us -> 588 us (0.930)
  Pallas kernels: 604 us -> 574 us
  local copies, waits for them, and re-layouts: 12.6 us -> 3.59 us
    pallas_call x1, Pallas kernels: 293 us -> 279 us  [call_backward(): pl.pallas_call(functools.partial(backward_kernel, heads), out_shape=[shap...]
    pallas_call x1, Pallas kernels: 195 us -> 183 us  [call_forward(): pl.pallas_call(functools.partial(forward_kernel, heads), out_shape=[shape...]
  transfers between devices with their start and end apart: 1 -> 0, of which waited for: 0 -> 0; matrix products, arithmetic and copies ran while one was open for 1% -> 0% of each run, Pallas kernels for 3% -> 0%
where the time goes in v2:
time: 588 us; the launch traced here: 583 us
  Pallas kernels  574 us (98%)
    pallas_call x1, Pallas kernels, call_backward(): pl.pallas_call(functools.partial(backward_kernel, heads), out_shape=[shap...  279 us
    pallas_call x1, Pallas kernels, call_forward(): pl.pallas_call(functools.partial(forward_kernel, heads), out_shape=[shape...  183 us
    pallas_call x1, Pallas kernels, call_middle(): pl.pallas_call(middle_kernel, out_shape=[shape((length, units), BF), shap...  91.3 us
    pallas_call x1, Pallas kernels, call_convert(): pl.pallas_call(convert_kernel, out_shape=[shape((slab, 4 * units), F32),...  20.6 us

profile of v2, /device:TPU:0, one launch (start us, length us, event | category | flops | bytes accessed | tf_op | source)
XLA Modules:
  0.0 582.8 jit_solution(10397823204838106213)
XLA Ops:
  0.7 0.7 fusion.2
  1.4 0.9 convert_reduce_fusion
  2.3 0.1 pad.14.clone
  2.4 0.7 broadcast_in_dim.6
  3.1 0.7 broadcast_in_dim.7
  3.8 0.7 maximum_convert_fusion.gains
  4.5 0.3 fusion
  4.8 0.7 pad_maximum_fusion.1.sin
  5.5 0.7 pad_maximum_fusion.cos
  6.2 0.8 and_convert_fusion.keep
  7.0 182.8 %attention_forward.1 = (bf16[128,1280]{1,0:T(8,128)(2,1)}, bf16[2,4,128,256]{3,2,1,0:T(8,128)(2,1)}, f32[5,128,512]{2,1,0:T(8,128)}, f32[64,2560]{1,0:T(8,128)},...) custom-call(bf16[128,2560]{1,0:T(8,128)(2,1)} %bitcast.19, ...), custom_call_target="tpu_custom_call" | custom-call | flops 1845493760 | bytes 400000000 | tf_op jit(solution)/shard_map/attention_forward/pallas_call | solution.py:858
  189.9 91.3 %feed_forward_backward.1 = (bf16[512,960]{1,0:T(8,128)(2,1)}, bf16[512,2560]{1,0:T(8,128)(2,1)}, bf16[512,2560]{1,0:T(8,128)(2,1)}, bf16[960,640]{1,0:T(8,128)(2,1)}, bf16[4,960,640]{2,1,0:T(8,128)(2,1)}) custom-call(bf16[3840,640]{1,0:T(8,128)(2,1)} %w_down.1, bf16[960,640]{1,0:T(8,128)(2,1)} %get-tuple-element.45.shard_down, bf16[512,2560]{1,0:T(8,128)(2,1)} %bitcast.28, ...), custom_call_target="tpu_custom_call" | custom-call | flops 15099494400 | bytes 300000000 | tf_op jit(solution)/shard_map/feed_forward_backward/pallas_call | solution.py:517
  281.2 279.3 %attention_backward.1 = (bf16[2,64,2560]{2,1,0:T(8,128)(2,1)}, f32[2,64,2560]{2,1,0:T(8,128)}, f32[8,640]{1,0:T(8,128)}, bf16[4,960,640]{2,1,0:T(8,128)(2,1)}, b...) custom-call(bf16[4,2,64,2560]{3,2,1,0:T(8,128)(2,1)} %bitcast.25, ...), custom_call_target="tpu_custom_call" | custom-call | flops 838860800 | bytes 300000000 | tf_op jit(solution)/shard_map/attention_backward/pallas_call | solution.py:1521
  560.5 1.4 slice_reduce_fusion
  561.9 20.6 %convert.4 = (f32[640,3840]{1,0:T(8,128)}, f32[640,3840]{1,0:T(8,128)}, f32[3840,640]{1,0:T(8,128)}, f32[1280,640]{1,0:T(8,128)}, f32[640,1280]{1,0:T(8,128)}, /...) custom-call(bf16[4,960,640]{2,1,0:T(8,128)(2,1)} %get-tuple-element.64.gate_all, ...), custom_call_target="tpu_custom_call" | custom-call | bytes 49152000 | tf_op jit(solution)/shard_map/convert/pallas_call | solution.py:1739
  (7 shorter events, 0.0 us)

commit v3 on v2

--- a/solution.py
+++ b/solution.py
@@ -489,17 +489,24 @@
     product.start()
     for p in range(PIECES // 2):
         spread.hand_far(p)
-    for j in range(4):
+
+    def turn_back(j, carry):
         block = jnp.dot(d_gate[...], gate_w[j], preferred_element_type=F32)
         block += jnp.dot(d_up[...], up_w[j], preferred_element_type=F32)
-        dn[:, j * slab : (j + 1) * slab] = block.astype(BF)
+        dn[:, lanes(j)] = block.astype(BF)
+        return carry
+
+    lax.fori_loop(0, 4, turn_back, 0)
     product.middle()
     for p in range(PIECES // 2, PIECES):
         spread.hand_far(p)
-    for j in range(4):
-        part[:, j * slab : (j + 1) * slab] = jnp.dot(
-            hidden[...], dfull[j], preferred_element_type=F32
-        ).astype(BF)
+
+    def feed(j, carry):
+        block = jnp.dot(hidden[...], dfull[j], preferred_element_type=F32)
+        part[:, lanes(j)] = block.astype(BF)
+        return carry
+
+    lax.fori_loop(0, 4, feed, 0)
     product.end()
     spread.close()
     wire.finish()
@@ -559,10 +566,10 @@
     heads,
     tok,
     cot,
-    gains,
-    cos,
-    sin,
-    keep,
+    seg,
+    freq,
+    gain_a,
+    gain_f,
     w_q,
     w_kv,
     w_o,
@@ -583,6 +590,8 @@
     upward,
     hidden,
     shard,
+    cos,
+    sin,
     xbuf,
     rbuf,
     part,
@@ -603,6 +612,7 @@
     near,
     far,
     sums,
+    keep,
     send,
     recv,
     local,
@@ -643,10 +653,12 @@
     x_in = [None] * 4
     for k in (1, 2, 3):
         x_in[k] = wire(tok.at[mine, lanes(fs[k])], xbuf.at[k, mine, :], "fsdp", fs[k])
+    grel[0] = jnp.zeros((8, slab), F32)
+    grel[0, 0:1, :] = gain_a[...].astype(F32)
+    grel[0, 1:2, :] = gain_f[...].astype(F32)
     g_in = [None] * 4
     for k in (1, 2, 3):
-        g_in[k] = wire(gains, grel.at[k], "fsdp", fs[k])
-    grel[0] = gains[...]
+        g_in[k] = wire(grel.at[0], grel.at[k], "fsdp", fs[k])
     xbuf[0] = tok[:, lanes(fs[0])]
     x = tok[...].astype(F32)
     r = lax.rsqrt(jnp.sum(x * x, axis=1, keepdims=True) * (1.0 / depth) + 1e-06)
@@ -686,7 +698,7 @@
             next(schedule, None)
 
     bulk(BULK[0])
-    gain_one = gains[0:1, :]
+    gain_one = grel[0, 0:1, :]
     kv_half = w_kv[:, pl.ds(pl.multiple_of(ti * HD, HD), HD)]
     p_in = [None] * 4
     pass_x = {}
@@ -708,6 +720,24 @@
         if k:
             p_in[k] = wire(part.at[k], precv.at[k], "fsdp", fs[k])
     bulk(BULK[1])
+
+    def segment(index):
+        at = pl.ds(pl.multiple_of(index * rows, rows), rows)
+        return jnp.broadcast_to(seg[:, at].astype(F32), (rows, rows))
+
+    mine_segment = segment(ci).T
+    row_index = lax.broadcasted_iota(jnp.int32, (rows, rows), 0) + ci * rows
+    lane = lax.broadcasted_iota(jnp.int32, (rows, rows), 1)
+    earlier = jnp.zeros((rows, 1), F32)
+    for k in range(4):
+        theirs = segment(cs[k])
+        earlier += jnp.sum(jnp.where(theirs < mine_segment, 1.0, 0.0), axis=1, keepdims=True)
+        inside = jnp.logical_and(theirs == mine_segment, lane + cs[k] * rows <= row_index)
+        keep[:, k * rows : (k + 1) * rows] = jnp.where(inside, 1.0, 0.0)
+    angle = (row_index.astype(F32) - earlier) * freq[...]
+    cos[...] = jnp.cos(angle)
+    turned = jnp.sin(angle)
+    sin[...] = jnp.where(lane < HD // 4, -turned, turned)
     for k in (1, 2, 3):
         p_in[k].wait_recv()
 
@@ -843,7 +873,7 @@
 BULK = (4, 5, 4, 4, 4, 7, 1)
 
 
-def call_forward(heads, tok, cot, gains, cos, sin, keep, w_q, w_kv, w_o, w_gate, w_up):
+def call_forward(heads, tok, cot, seg, freq, gain_a, gain_f, w_q, w_kv, w_o, w_gate, w_up):
     rows, depth = tok.shape
     slab, hrows, qcols, length = depth // 4, rows // 2, heads * HD, 4 * rows
     units = w_gate.shape[1] // 4
@@ -873,9 +903,11 @@
             shape((length, units), F32),
             shape((length, units), BF),
             shape((units, slab), BF),
+            shape((rows, 128), F32),
+            shape((rows, 128), F32),
         ],
         in_specs=[vmem] * 9 + [hbm] * 2,
-        out_specs=[vmem] * 5 + [hbm] * 4 + [vmem] * 6,
+        out_specs=[vmem] * 5 + [hbm] * 4 + [vmem] * 8,
         scratch_shapes=[
             pltpu.VMEM((4, rows, slab), BF),
             pltpu.VMEM((4, rows, 128), F32),
@@ -897,6 +929,7 @@
             list(pair),
             list(single),
             list(single),
+            pltpu.VMEM((rows, length), F32),
             pltpu.SemaphoreType.DMA((132,)),
             pltpu.SemaphoreType.DMA((132,)),
             pltpu.SemaphoreType.DMA((12,)),
@@ -908,7 +941,7 @@
             flops=2 * length * slab * (2 * qcols + HD), bytes_accessed=400_000_000, transcendentals=0
         ),
         name="attention_forward",
-    )(tok, cot, gains, cos, sin, keep, w_q, w_kv, w_o, w_gate, w_up)
+    )(tok, cot, seg, freq, gain_a, gain_f, w_q, w_kv, w_o, w_gate, w_up)
 
 
 class Product:
@@ -1470,9 +1503,9 @@
     last.lead()
     for p in range(PIECES):
         weight_line.hand_on(p)
-    last.push_near()
     for p in range(PIECES // 2):
         weight_line.hand_far(p)
+    last.push_near()
     last.push_far()
     for p in range(PIECES // 2, PIECES):
         weight_line.hand_far(p)
@@ -1785,7 +1818,6 @@
     gain_ffn,
     cotangent,
 ):
-    ci = lax.axis_index("ctx")
     tok, cot = tokens[0], cotangent[0]
     rows, depth = tok.shape
     hrows, slab = rows // 2, depth // 4
@@ -1793,30 +1825,8 @@
     heads = w_query.shape[1] // HD
     units = w_gate.shape[1] // 4
 
-    def cut(value, start, size, axis):
-        return lax.dynamic_slice_in_dim(value, start, size, axis)
-
-    segment_row = segment_ids[0]
-    local_segment = cut(segment_row, ci * rows, rows, 0)
-    local_index = ci * rows + jnp.arange(rows, dtype=jnp.int32)
-    earlier = jnp.sum((segment_row[None, :] < local_segment[:, None]).astype(jnp.int32), axis=1)
-    position = (local_index - earlier).astype(F32)
     freqs = 10000.0 ** (-(jnp.arange(HD // 4, dtype=F32) * 2.0 / (HD // 2)))
-    angle = position[:, None] * freqs[None, :]
-    cosine, sine = jnp.cos(angle), jnp.sin(angle)
-    cos = jnp.concatenate([cosine, cosine], axis=1)
-    sin = jnp.concatenate([-sine, sine], axis=1)
-    key_index = jnp.concatenate(
-        [(ci ^ k) * rows + jnp.arange(rows, dtype=jnp.int32) for k in range(4)]
-    )
-    key_segment = jnp.concatenate([cut(segment_row, (ci ^ k) * rows, rows, 0) for k in range(4)])
-    keep = (
-        (local_segment[:, None] == key_segment[None, :])
-        & (key_index[None, :] <= local_index[:, None])
-    ).astype(F32)
-    gains = jnp.concatenate(
-        [gain_attn[None], gain_ffn[None], jnp.zeros((6, slab), gain_attn.dtype)]
-    ).astype(F32)
+    freqs = jnp.concatenate([freqs, freqs])[None]
 
     (
         q_rot,
@@ -1834,14 +1844,16 @@
         upward,
         hidden,
         shard_down,
+        cos,
+        sin,
     ) = call_forward(
         heads,
         tok,
         cot,
-        gains,
-        cos,
-        sin,
-        keep,
+        segment_ids,
+        freqs,
+        gain_attn[None],
+        gain_ffn[None],
         w_query,
         w_keyval,
         w_out,
@@ -1940,7 +1952,7 @@
 
     def body(*args):
         rows, depth = args[0].shape[1:]
-        fits = sizes == (4, 4, 2) and depth % 512 == 0 and rows % 32 == 0
+        fits = sizes == (4, 4, 2) and depth % 512 == 0 and rows == 128
         if fits:
             return fast_device(*args)
         return per_device(sizes, *args)

time: 588 us -> 585 us (level)
  no operation moved by 1% of the time
where the time goes in v3:
time: 585 us; the launch traced here: 580 us
  Pallas kernels  574 us (98%)
    pallas_call x1, Pallas kernels, call_backward(): pl.pallas_call(functools.partial(backward_kernel, heads), out_shape=[shap...  280 us
    pallas_call x1, Pallas kernels, call_forward(): pl.pallas_call(functools.partial(forward_kernel, heads), out_shape=[shape...  183 us
    pallas_call x1, Pallas kernels, call_middle(): pl.pallas_call(middle_kernel, out_shape=[shape((length, units), BF), shap...  91.3 us
    pallas_call x1, Pallas kernels, call_convert(): pl.pallas_call(convert_kernel, out_shape=[shape((slab, 4 * units), F32),...  20.6 us

profile of v3, /device:TPU:0, one launch (start us, length us, event | category | flops | bytes accessed | tf_op | source)
XLA Modules:
  0.0 580.0 jit_solution(5459532371459898704)
XLA Ops:
  0.7 0.6 maximum_bitcast_fusion.freq
  1.2 1.3 broadcast_in_dim.10.gain_a
  2.5 1.3 broadcast_in_dim.11.gain_f
  3.8 182.8 %attention_forward.1 = (bf16[128,1280]{1,0:T(8,128)(2,1)}, bf16[2,4,128,256]{3,2,1,0:T(8,128)(2,1)}, f32[5,128,512]{2,1,0:T(8,128)}, f32[64,2560]{1,0:T(8,128)},...) custom-call(bf16[128,2560]{1,0:T(8,128)(2,1)} %bitcast.12, ...), custom_call_target="tpu_custom_call" | custom-call | flops 1845493760 | bytes 400000000 | tf_op jit(solution)/shard_map/attention_forward/pallas_call | solution.py:888
  186.6 91.3 %feed_forward_backward.1 = (bf16[512,960]{1,0:T(8,128)(2,1)}, bf16[512,2560]{1,0:T(8,128)(2,1)}, bf16[512,2560]{1,0:T(8,128)(2,1)}, bf16[960,640]{1,0:T(8,128)(2,1)}, bf16[4,960,640]{2,1,0:T(8,128)(2,1)}) custom-call(bf16[3840,640]{1,0:T(8,128)(2,1)} %w_down.1, bf16[960,640]{1,0:T(8,128)(2,1)} %get-tuple-element.47.shard_down, bf16[512,2560]{1,0:T(8,128)(2,1)} %bitcast.20, ...), custom_call_target="tpu_custom_call" | custom-call | flops 15099494400 | bytes 300000000 | tf_op jit(solution)/shard_map/feed_forward_backward/pallas_call | solution.py:524
  277.9 279.7 %attention_backward.1 = (bf16[2,64,2560]{2,1,0:T(8,128)(2,1)}, f32[2,64,2560]{2,1,0:T(8,128)}, f32[8,640]{1,0:T(8,128)}, bf16[4,960,640]{2,1,0:T(8,128)(2,1)}, b...) custom-call(bf16[4,2,64,2560]{3,2,1,0:T(8,128)(2,1)} %bitcast.18, ...), custom_call_target="tpu_custom_call" | custom-call | flops 838860800 | bytes 300000000 | tf_op jit(solution)/shard_map/attention_backward/pallas_call | solution.py:1554
  557.7 1.4 slice_reduce_fusion
  559.1 20.6 %convert.1 = (f32[640,3840]{1,0:T(8,128)}, f32[640,3840]{1,0:T(8,128)}, f32[3840,640]{1,0:T(8,128)}, f32[1280,640]{1,0:T(8,128)}, f32[640,1280]{1,0:T(8,128)}, /...) custom-call(bf16[4,960,640]{2,1,0:T(8,128)(2,1)} %get-tuple-element.68.gate_all, ...), custom_call_target="tpu_custom_call" | custom-call | bytes 49152000 | tf_op jit(solution)/shard_map/convert/pallas_call | solution.py:1772
  (1 shorter events, 0.0 us)
